TPU v7x, 512 devices: a whole 4x4x16 slice. The times are simulated.
512 devices in a mesh: row: 16 (over x, y), col: 32 (over z, core).
Axes of the slice: x: 4, y: 4, z: 16, core: 2. Of those that a mesh axis runs over, the one named last changes fastest.
Arguments:
- factors: float32 [1, 8192, 8192], P(None, 'row', 'col'), may hold values from -20 to 30, as said below
Outputs:
- refreshed: float32 [1, 8192, 8192], P(None, 'row', 'col')
Inputs may be any that keep to these rules, and one draw needn't show every extreme that they name: `factors`: every factor is symmetric positive definite.
All inputs are finite; a program needn't handle non-finite values.
Results may differ from a plain program's by a relative error of at most 0.0003.
Values sent between devices are 32-bit elements; how exact they have to be, the bound alone decides.
A program may use at most 64 MiB of HBM per device.

v0:
```python
import jax
import jax.numpy as jnp
from jax import lax
from jax.sharding import Mesh
from jax.sharding import PartitionSpec as P

P_SIZE = 512
STEPS = 2
COL = ("col_0", "col_1")
ROW = ("row_0", "row_1")
ROW_COL = ("row_0", "row_1", "col_0", "col_1")


damping_share = 0.03162277660168379
top_precision = lax.Precision.HIGHEST


def one_axis_at_a_time(x, axes):
    for axis in axes:
        x = lax.psum(x, axis)
    return x


def laid_out(parts, dim):
    parts = jnp.moveaxis(parts, 0, dim)
    dims = parts.shape
    return parts.reshape(*dims[:dim], dims[dim] * dims[dim + 1], *dims[dim + 2 :])


def from_everyone(x, axis):
    copies = jnp.broadcast_to(x, (lax.axis_size(axis), *x.shape))
    return lax.all_to_all(copies, axis, split_axis=0, concat_axis=0, tiled=True)


def gather_directly(x, axis, dim):
    return laid_out(from_everyone(x, axis), dim)


def on_device(factors):
    members, rows_dev, cols_dev = factors.shape
    col_count = lax.axis_size(COL)
    order = rows_dev * lax.axis_size(ROW)
    row_id = lax.axis_index(ROW)
    col_id = lax.axis_index(COL)
    blocks_per_row = rows_dev // cols_dev
    panel_slab = P_SIZE // col_count
    diag_height = blocks_per_row * panel_slab
    row_global = row_id * rows_dev + jnp.arange(rows_dev, dtype=jnp.int32)
    col_global = col_id * cols_dev + jnp.arange(cols_dev, dtype=jnp.int32)
    row_panel = row_global % cols_dev // panel_slab
    col_panel = col_global % cols_dev // panel_slab
    on_diagonal = (row_global[:, None] == col_global[None, :])[None]
    local_trace = jnp.sum(jnp.where(on_diagonal, factors, 0.0), axis=(1, 2))
    full_trace = one_axis_at_a_time(local_trace, ROW_COL)
    working = factors + jnp.where(
        on_diagonal, (damping_share * full_trace / order)[:, None, None], 0.0
    )
    identity = jnp.broadcast_to(jnp.eye(P_SIZE, dtype=jnp.float32), (members, P_SIZE, P_SIZE))
    for section_no in range(STEPS):
        col_first = section_no * panel_slab
        panel_cols = working[:, :, col_first : col_first + panel_slab]
        diag_piece = panel_cols.reshape(members, blocks_per_row, cols_dev, panel_slab)
        diag_piece = diag_piece[:, :, col_first : col_first + panel_slab, :].reshape(
            members, diag_height, panel_slab
        )
        row_strip = gather_directly(diag_piece, COL, 2)
        diag_block = gather_directly(row_strip, ROW, 1)
        factor_kk = jnp.linalg.cholesky(diag_block)
        inverse_kk = jax.scipy.linalg.solve_triangular(factor_kk, identity, lower=True)
        solve_w = jnp.swapaxes(inverse_kk, 1, 2)
        lower_rows = jnp.einsum(
            "fij,fjq->fiq", gather_directly(panel_cols, COL, 2), solve_w, precision=top_precision
        )
        upper_rows = working.reshape(members, blocks_per_row, cols_dev, cols_dev)
        upper_rows = upper_rows[:, :, col_first : col_first + panel_slab, :].reshape(
            members, diag_height, cols_dev
        )
        cross_rows = jnp.einsum(
            "fpj,fpq->fjq", gather_directly(upper_rows, ROW, 1), solve_w, precision=top_precision
        )
        syrk_term = jnp.einsum("fiq,fjq->fij", lower_rows, cross_rows, precision=top_precision)
        trailing = ((row_panel > section_no)[:, None] & (col_panel > section_no)[None, :])[None]
        working = jnp.where(trailing, working - syrk_term, working)
        new_columns = lax.dynamic_slice_in_dim(lower_rows, col_id * panel_slab, panel_slab, 2)
        chol_rows = lax.dynamic_slice_in_dim(factor_kk, row_id * diag_height, diag_height, 1)
        chol_rows = lax.dynamic_slice_in_dim(chol_rows, col_id * panel_slab, panel_slab, 2)
        new_columns = new_columns.reshape(members, blocks_per_row, cols_dev, panel_slab)
        new_columns = new_columns.at[:, :, col_first : col_first + panel_slab, :].set(
            chol_rows.reshape(members, blocks_per_row, panel_slab, panel_slab)
        )
        new_columns = new_columns.reshape(members, rows_dev, panel_slab)
        old_columns = working[:, :, col_first : col_first + panel_slab]
        new_columns = jnp.where((row_panel >= section_no)[None, :, None], new_columns, old_columns)
        working = working.at[:, :, col_first : col_first + panel_slab].set(new_columns)
        upper_mask = ((row_panel == section_no)[:, None] & (col_panel > section_no)[None, :])[None]
        working = jnp.where(upper_mask, 0.0, working)
    return working


def solution(mesh):
    torus = Mesh(mesh.devices.reshape(4, 4, 16, 2), ("row_0", "row_1", "col_0", "col_1"))
    placed = (P(None, ROW, COL),)
    return jax.shard_map(
        on_device, mesh=torus, in_specs=placed, out_specs=P(None, ROW, COL), check_vma=False
    )
```

profile of v0, /device:TPU:1, one launch (start us, length us, event | category | flops | bytes accessed | tf_op | source)
XLA Modules:
  0.0 508.9 jit_solution(11446738001307668075)
XLA Ops:
  0.0 1.2 copy.52
  2.1 9.9 %psum.28 = f32[1]{0:T(128)} all-reduce(f32[1]{0:T(128)} %bitcast), channel_id=1, replica_groups=mesh['row_0'=4,'row_1'=4,'col_0'=16,'col_1'=2] {'row_0'}, use_global_device_ids=true, to_apply=%region_1.2 | all-reduce | flops 1 | bytes 8 | tf_op jit(solution)/shard_map/psum | solution.py:20
  12.0 9.3 %psum.29 = f32[1]{0:T(128)} all-reduce(f32[1]{0:T(128)} %psum.28), channel_id=1, replica_groups=mesh['row_0'=4,'row_1'=4,'col_0'=16,'col_1'=2] {'row_1'}, use_global_device_ids=true, to_apply=%region_2.3 | all-reduce | flops 1 | bytes 8 | tf_op jit(solution)/shard_map/psum | solution.py:20
  21.3 30.4 %psum.30 = f32[1]{0:T(128)} all-reduce(f32[1]{0:T(128)} %psum.29), channel_id=1, replica_groups=mesh['row_0'=4,'row_1'=4,'col_0'=16,'col_1'=2] {'col_0'}, use_global_device_ids=true, to_apply=%region_3.4 | all-reduce | flops 1 | bytes 8 | tf_op jit(solution)/shard_map/psum | solution.py:20
  51.6 14.2 %psum.31 = f32[1]{0:T(128)} all-reduce(f32[1]{0:T(128)} %psum.30), channel_id=1, replica_groups=mesh['row_0'=4,'row_1'=4,'col_0'=16,'col_1'=2] {'col_1'}, use_global_device_ids=true, to_apply=%region_4.5 | all-reduce | flops 1 | bytes 8 | tf_op jit(solution)/shard_map/psum | solution.py:20
  67.0 19.9 %all_to_all.40 = f32[32,1,512]{2,1,0:T(1,128)S(1)} all-to-all(f32[32,1,512]{2,1,0:T(1,128)S(1)} %reshape.846), channel_id=1, replica_groups=mesh['row_0'=4,'row_1'=4,'col_0'=16,'col_1'=2] {'col_0','col_1'}, dimensions={0} | all-to-all | bytes 131072 | tf_op jit(solution)/shard_map/all_to_all | solution.py:32
  89.4 3.7 all-to-all-start.2
  93.5 14.9 %all-to-all-done.2 = f32[16,1,32,512]{3,2,1,0:T(8,128)S(1)} async-done(((f32[16,1,32,512]{3,2,1,0:T(8,128)}), f32[16,1,32,512]{3,2,1,0:T(8,128)S(1)}, u32[]{:S(2)}, u32[]{:S(2)}) %all-to-all-start.2) | async-done | bytes 1048608 | tf_op jit(solution)/shard_map/all_to_all | solution.py:32
  109.3 4.5 all-to-all-start.3
  113.7 1.3 copy.55
  115.1 1.4 fusion.15
  117.5 11.7 %custom-call.35 = f32[1,128,128]{2,1,0:T(8,128)S(1)} custom-call(f32[1,128,128]{2,1,0:T(8,128)S(1)} %cholesky.425), custom_call_target="Cholesky" | custom-call | tf_op jit(solution)/shard_map/jit(cholesky)/cholesky | solution.py:68
  129.3 9.8 %custom-call.36 = f32[1,1,128,128]{2,3,1,0:T(8,128)S(1)} custom-call(f32[1,1,128,128]{3,2,1,0:T(8,128)S(1)} %get-tuple-element.118), custom_call_target="InvertDiagBlocksLowerTriangular" | custom-call | tf_op jit(solution)/shard_map/jit(cholesky)/cholesky | solution.py:68
  139.1 1.3 fusion.44
  140.7 1.4 fusion.4
  142.2 11.7 %custom-call.37 = f32[1,128,128]{2,1,0:T(8,128)S(1)} custom-call(f32[1,128,128]{2,1,0:T(8,128)S(1)} %cholesky.429), custom_call_target="Cholesky" | custom-call | tf_op jit(solution)/shard_map/jit(cholesky)/cholesky | solution.py:68
  153.9 10.2 %custom-call.38 = f32[1,1,128,128]{2,3,1,0:T(8,128)S(1)} custom-call(f32[1,1,128,128]{3,2,1,0:T(8,128)S(1)} %get-tuple-element.115), custom_call_target="InvertDiagBlocksLowerTriangular" | custom-call | tf_op jit(solution)/shard_map/jit(cholesky)/cholesky | solution.py:68
  164.4 1.3 fusion.8
  165.7 11.7 %custom-call.39 = f32[1,128,128]{2,1,0:T(8,128)S(1)} custom-call(f32[1,128,128]{2,1,0:T(8,128)S(1)} %cholesky.434), custom_call_target="Cholesky" | custom-call | tf_op jit(solution)/shard_map/jit(cholesky)/cholesky | solution.py:68
  178.1 9.8 %custom-call.40 = f32[1,1,128,128]{2,3,1,0:T(8,128)S(1)} custom-call(f32[1,1,128,128]{3,2,1,0:T(8,128)S(1)} %get-tuple-element.112), custom_call_target="InvertDiagBlocksLowerTriangular" | custom-call | tf_op jit(solution)/shard_map/jit(cholesky)/cholesky | solution.py:68
  190.5 7.2 %all-to-all-start = ((f32[32,1,512,16]{2,3,1,0:T(8,128)}), f32[32,1,512,16]{2,3,1,0:T(8,128)}, u32[]{:S(2)}, u32[]{:S(2)}) async-start(f32[32,1,512,16]{2,3,1,0:T(8,128)} %broadcast_in_dim.83), calls=%async_computation | async-start | bytes 2097152 | tf_op jit(solution)/shard_map/all_to_all | solution.py:32
  198.4 11.7 %custom-call.41 = f32[1,128,128]{2,1,0:T(8,128)S(1)} custom-call(f32[1,128,128]{2,1,0:T(8,128)S(1)} %fusion.12), custom_call_target="Cholesky" | custom-call | tf_op jit(solution)/shard_map/jit(cholesky)/cholesky | solution.py:68
  213.3 1.6 bitcast_select_fusion.1
  214.9 11.9 %while.8 = (s32[]{:T(128)}, f32[512,512]{1,0:T(8,128)}, s32[4,2]{0,1:T(2,128)S(1)}, f32[4,128,128]{2,1,0:T(8,128)S(1)}, s32[]{:T(128)}) while((s32[]{:T(128)}, f32[512,512]{1,0:T(8,128)}, s32[4,2]{0,1:T(2,128)S(1)}, f32[4,128,128]{2,1,0:T(8,128)S(1)}, s32[]{:T(128)}) %tuple.72), condition=%wide.while_cond.4, body=%wide.while_body.4.sunk | while | flops 2 | bytes 131181 | solution.py:69
  215.6 2.3 bitcast_dynamic-update-slice_fusion.4
  218.6 2.3 bitcast_dynamic-update-slice_fusion.4
  221.6 2.3 bitcast_dynamic-update-slice_fusion.4
  224.6 2.3 bitcast_dynamic-update-slice_fusion.4
  226.8 39.5 %custom-call.42 = f32[4,128,128]{1,2,0:T(8,128)S(1)} custom-call(f32[4,128,128]{2,1,0:T(8,128)S(1)} %get-tuple-element.69), custom_call_target="InvertDiagBlocksLowerTriangular" | custom-call | tf_op jit(solution)/shard_map/jit(_solve_triangular)/triangular_solve | solution.py:69
  269.3 1.3 convolution_subtract_fusion.2
  271.1 1.6 convolution_subtract_fusion.5
  273.1 3.8 fusion.30
  276.9 3.1 fusion.29
  280.5 2.1 fusion.1
  283.2 25.1 %all_to_all.41 = f32[32,1,512]{2,1,0:T(1,128)S(1)} all-to-all(f32[32,1,512]{2,1,0:T(1,128)S(1)} %reshape.848), channel_id=1, replica_groups=mesh['row_0'=4,'row_1'=4,'col_0'=16,'col_1'=2] {'col_0','col_1'}, dimensions={0} | all-to-all | bytes 131072 | tf_op jit(solution)/shard_map/all_to_all | solution.py:32
  310.3 6.8 %all-to-all-start.6 = ((f32[16,1,32,512]{3,2,1,0:T(8,128)}), f32[16,1,32,512]{3,2,1,0:T(8,128)S(1)}, u32[]{:S(2)}, u32[]{:S(2)}) async-start(f32[16,1,32,512]{3,2,1,0:T(8,128)} %broadcast_in_dim.90), calls=%async_computation.6 | async-start | bytes 2097152 | tf_op jit(solution)/shard_map/all_to_all | solution.py:32
  317.4 14.9 %all-to-all-done.6 = f32[16,1,32,512]{3,2,1,0:T(8,128)S(1)} async-done(((f32[16,1,32,512]{3,2,1,0:T(8,128)}), f32[16,1,32,512]{3,2,1,0:T(8,128)S(1)}, u32[]{:S(2)}, u32[]{:S(2)}) %all-to-all-start.6) | async-done | bytes 1048608 | tf_op jit(solution)/shard_map/all_to_all | solution.py:32
  333.1 4.4 all-to-all-start.7
  337.6 1.3 copy.63
  338.9 1.4 fusion.14
  341.4 11.7 %custom-call.43 = f32[1,128,128]{2,1,0:T(8,128)S(1)} custom-call(f32[1,128,128]{2,1,0:T(8,128)S(1)} %cholesky.438), custom_call_target="Cholesky" | custom-call | tf_op jit(solution)/shard_map/jit(cholesky)/cholesky | solution.py:68
  353.2 9.8 %custom-call.44 = f32[1,1,128,128]{2,3,1,0:T(8,128)S(1)} custom-call(f32[1,1,128,128]{3,2,1,0:T(8,128)S(1)} %get-tuple-element.108), custom_call_target="InvertDiagBlocksLowerTriangular" | custom-call | tf_op jit(solution)/shard_map/jit(cholesky)/cholesky | solution.py:68
  363.1 1.3 fusion.42
  364.6 1.4 fusion.5
  366.0 11.7 %custom-call.45 = f32[1,128,128]{2,1,0:T(8,128)S(1)} custom-call(f32[1,128,128]{2,1,0:T(8,128)S(1)} %cholesky.442), custom_call_target="Cholesky" | custom-call | tf_op jit(solution)/shard_map/jit(cholesky)/cholesky | solution.py:68
  378.4 10.2 %custom-call.46 = f32[1,1,128,128]{2,3,1,0:T(8,128)S(1)} custom-call(f32[1,1,128,128]{3,2,1,0:T(8,128)S(1)} %get-tuple-element.105), custom_call_target="InvertDiagBlocksLowerTriangular" | custom-call | tf_op jit(solution)/shard_map/jit(cholesky)/cholesky | solution.py:68
  388.9 1.3 fusion.9
  390.2 11.7 %custom-call.47 = f32[1,128,128]{2,1,0:T(8,128)S(1)} custom-call(f32[1,128,128]{2,1,0:T(8,128)S(1)} %cholesky.447), custom_call_target="Cholesky" | custom-call | tf_op jit(solution)/shard_map/jit(cholesky)/cholesky | solution.py:68
  402.6 9.8 %custom-call.48 = f32[1,1,128,128]{2,3,1,0:T(8,128)S(1)} custom-call(f32[1,1,128,128]{3,2,1,0:T(8,128)S(1)} %get-tuple-element.102), custom_call_target="InvertDiagBlocksLowerTriangular" | custom-call | tf_op jit(solution)/shard_map/jit(cholesky)/cholesky | solution.py:68
  412.6 1.2 fusion.13
  415.0 7.6 %all-to-all-start.4 = ((f32[32,1,512,16]{2,3,1,0:T(8,128)}), f32[32,1,512,16]{2,3,1,0:T(8,128)}, u32[]{:S(2)}, u32[]{:S(2)}) async-start(f32[32,1,512,16]{2,3,1,0:T(8,128)} %broadcast_in_dim.88), calls=%async_computation.4 | async-start | bytes 2097152 | tf_op jit(solution)/shard_map/all_to_all | solution.py:32
  423.2 11.7 %custom-call.49 = f32[1,128,128]{2,1,0:T(8,128)S(1)} custom-call(f32[1,128,128]{2,1,0:T(8,128)S(1)} %fusion.13), custom_call_target="Cholesky" | custom-call | tf_op jit(solution)/shard_map/jit(cholesky)/cholesky | solution.py:68
  438.2 1.6 bitcast_select_fusion
  439.8 11.8 %while.9 = (s32[]{:T(128)}, f32[512,512]{1,0:T(8,128)}, s32[4,2]{0,1:T(2,128)S(1)}, f32[4,128,128]{2,1,0:T(8,128)S(1)}, s32[]{:T(128)}) while((s32[]{:T(128)}, f32[512,512]{1,0:T(8,128)}, s32[4,2]{0,1:T(2,128)S(1)}, f32[4,128,128]{2,1,0:T(8,128)S(1)}, s32[]{:T(128)}) %tuple.78), condition=%wide.while_cond.4.clone, body=%wide.while_body.4.clone.sunk | while | flops 2 | bytes 131181 | solution.py:69
  440.4 2.3 bitcast_dynamic-update-slice_fusion.5
  443.4 2.3 bitcast_dynamic-update-slice_fusion.5
  446.3 2.3 bitcast_dynamic-update-slice_fusion.5
  449.3 2.2 bitcast_dynamic-update-slice_fusion.5
  451.5 39.5 %custom-call.50 = f32[4,128,128]{1,2,0:T(8,128)S(1)} custom-call(f32[4,128,128]{2,1,0:T(8,128)S(1)} %get-tuple-element.70), custom_call_target="InvertDiagBlocksLowerTriangular" | custom-call | tf_op jit(solution)/shard_map/jit(_solve_triangular)/triangular_solve | solution.py:69
  494.1 1.3 convolution_subtract_fusion
  495.8 1.6 convolution_subtract_fusion.4
  497.8 2.9 fusion.28
  500.7 3.1 fusion.27
  503.9 2.5 scatter.16
  (128 shorter events, 36.1 us)
Async XLA Ops:
  89.4 19.0 %all-to-all-start.2 = ((f32[16,1,32,512]{3,2,1,0:T(8,128)}), f32[16,1,32,512]{3,2,1,0:T(8,128)S(1)}, u32[]{:S(2)}, u32[]{:S(2)}) async-start(f32[16,1,32,512]{3,2,1,0:T(8,128)} %broadcast_in_dim.85), calls=%async_computation.2 | async-start | bytes 2097152 | tf_op jit(solution)/shard_map/all_to_all | solution.py:32
  109.3 80.1 %all-to-all-start.3 = ((f32[16,1,32,256]{3,2,1,0:T(8,128)}), f32[16,1,32,256]{3,2,1,0:T(8,128)}, u32[]{:S(2)}, u32[]{:S(2)}) async-start(f32[16,1,32,256]{3,2,1,0:T(8,128)} %broadcast_in_dim.86), calls=%async_computation.3 | async-start | bytes 1048576 | tf_op jit(solution)/shard_map/all_to_all | solution.py:32
  116.5 1.0 copy-start
  190.5 86.4 %all-to-all-start = ((f32[32,1,512,16]{2,3,1,0:T(8,128)}), f32[32,1,512,16]{2,3,1,0:T(8,128)}, u32[]{:S(2)}, u32[]{:S(2)}) async-start(f32[32,1,512,16]{2,3,1,0:T(8,128)} %broadcast_in_dim.83), calls=%async_computation | async-start | bytes 2097152 | tf_op jit(solution)/shard_map/all_to_all | solution.py:32
  273.1 3.8 copy-start.2
  310.3 21.9 %all-to-all-start.6 = ((f32[16,1,32,512]{3,2,1,0:T(8,128)}), f32[16,1,32,512]{3,2,1,0:T(8,128)S(1)}, u32[]{:S(2)}, u32[]{:S(2)}) async-start(f32[16,1,32,512]{3,2,1,0:T(8,128)} %broadcast_in_dim.90), calls=%async_computation.6 | async-start | bytes 2097152 | tf_op jit(solution)/shard_map/all_to_all | solution.py:32
  333.1 80.7 %all-to-all-start.7 = ((f32[16,1,32,256]{3,2,1,0:T(8,128)}), f32[16,1,32,256]{3,2,1,0:T(8,128)}, u32[]{:S(2)}, u32[]{:S(2)}) async-start(f32[16,1,32,256]{3,2,1,0:T(8,128)} %broadcast_in_dim.91), calls=%async_computation.7 | async-start | bytes 1048576 | tf_op jit(solution)/shard_map/all_to_all | solution.py:32
  340.4 1.0 copy-start.1
  415.0 85.8 %all-to-all-start.4 = ((f32[32,1,512,16]{2,3,1,0:T(8,128)}), f32[32,1,512,16]{2,3,1,0:T(8,128)}, u32[]{:S(2)}, u32[]{:S(2)}) async-start(f32[32,1,512,16]{2,3,1,0:T(8,128)} %broadcast_in_dim.88), calls=%async_computation.4 | async-start | bytes 2097152 | tf_op jit(solution)/shard_map/all_to_all | solution.py:32
where the time goes:
time: 514 us; the launch traced here: 509 us
  other arithmetic  246 us (48%)
  blocking collectives  109 us (21%)
  local copies, waits for them, and re-layouts  44.1 us (9%)
  matrix products  39.1 us (8%)
  starting transfers between devices  34.2 us (7%)
  waiting for transfers between devices  29.8 us (6%)
  between operations  6.76 us (1%)
    another operation x29, other arithmetic, on_device(): factor_kk = jnp.linalg.cholesky(diag_block)  158 us
    another operation x5, other arithmetic, on_device(): jax.scipy.linalg.solve_triangular(factor_kk, identity, lower=True)  82.2 us
    psum x4, blocking collectives, one_axis_at_a_time(): x = lax.psum(x, axis)  63.8 us
    all_to_all x2, blocking collectives, from_everyone(): return lax.all_to_all(copies, axis, split_axis=0, concat_axis=0, tiled=True)  45 us
    all_to_all x6, starting transfers between devices, from_everyone(): return lax.all_to_all(copies, axis, split_axis=0, concat_axis=0, tiled=True)  34.2 us
    all_to_all x6, waiting for transfers between devices, from_everyone(): return lax.all_to_all(copies, axis, split_axis=0, concat_axis=0, tiled=True)  29.8 us
    another operation x27, local copies, waits for them, and re-layouts, on_device(): jax.scipy.linalg.solve_triangular(factor_kk, identity, lower=True)  23.5 us
    another operation x14, matrix products, on_device(): jax.scipy.linalg.solve_triangular(factor_kk, identity, lower=True)  11.5 us
  transfers between devices with their start and end apart: 6, of which 2 were waited for; matrix products, arithmetic and copies ran while one was open for 59% of the time, Pallas kernels for 0%

commit v1 on v0

v1 whole, which is shorter than its diff:
```python
import jax, jax.numpy as jnp
from jax import lax
from jax.experimental import pallas as pl
from jax.experimental.pallas import tpu as pltpu
from jax.sharding import PartitionSpec as P

F32, BF16 = jnp.float32, jnp.bfloat16
damping_share = 0.03162277660168379

def split3(x):
    h = x.astype(BF16)
    r = x - h.astype(F32)
    m = r.astype(BF16)
    l = (r - m.astype(F32)).astype(BF16)
    return h, m, l

def split2(x):
    h = x.astype(BF16)
    return h, (x - h.astype(F32)).astype(BF16)

def tn(a, b):
    return lax.dot_general(a, b, (((0,), (0,)), ((), ())), preferred_element_type=F32)

def nn(a, b):
    return lax.dot_general(a, b, (((1,), (0,)), ((), ())), preferred_element_type=F32)

def block_inverse(M, b=16):
    n = 128
    H = b // 8
    sub = lax.broadcasted_iota(jnp.int32, (8, n), 0)
    lane = lax.broadcasted_iota(jnp.int32, (8, n), 1)
    M = [M[8 * i:8 * i + 8, :] for i in range(n // 8)]
    for s in range(n // b):
        r0 = s * b
        q0 = r0 // 8
        S = [[None] * b for _ in range(H)]
        for k in range(b):
            for h in range(k // 8, H):
                S[h][k] = jnp.broadcast_to(M[q0 + h][:, r0 + k:r0 + k + 1], (8, n))
        inblk = (lane >= r0) & (lane < r0 + b)
        N = [jnp.where(inblk, jnp.where(lane - r0 == sub + 8 * h, 1.0, 0.0).astype(F32), M[q0 + h]) for h in range(H)]
        scale = [None] * H
        for j in range(b):
            hj, sj = j // 8, j % 8
            piv = jnp.broadcast_to(S[hj][j][sj:sj + 1, :], (8, n))
            rs = lax.rsqrt(piv)
            rinv = rs * rs
            scale[hj] = rs if sj == 0 else jnp.where(sub == sj, rs, scale[hj])
            if j == b - 1:
                break
            for k in range(j + 1, b):
                hk, sk = k // 8, k % 8
                t = jnp.broadcast_to(S[hk][j][sk:sk + 1, :], (8, n)) * rinv
                for h in range(hk, H):
                    S[h][k] = S[h][k] - S[h][j] * t
            prow = jnp.broadcast_to(N[hj][sj:sj + 1, :], (8, n)) * rinv
            for h in range(hj, H):
                if h == hj:
                    if sj == 7:
                        continue
                    N[h] = jnp.where(sub > sj, N[h] - S[h][j] * prow, N[h])
                else:
                    N[h] = N[h] - S[h][j] * prow
        Y = jnp.concatenate([N[h] * scale[h] for h in range(H)], axis=0)
        lb = lax.broadcasted_iota(jnp.int32, (b, n), 1)
        for h in range(H):
            M[q0 + h] = Y[8 * h:8 * h + 8, :] if s == n // b - 1 else jnp.where(lane < r0 + b, Y[8 * h:8 * h + 8, :], 0.0)
        if s < n // b - 1:
            h_, m_, l_ = split3(Y)
            R = tn(jnp.concatenate([h_, h_, m_, h_, l_, m_], 0), jnp.concatenate([h_, m_, h_, l_, h_, m_], 0))
            for q in range(q0 + H, n // 8):
                M[q] = jnp.where(inblk, 0.0, M[q]) - R[8 * q:8 * q + 8, :]
    return jnp.concatenate(M, axis=0)

NBLK = 8
NB = 128
KK = 1024
LB = 768

def cat3l(h, l):
    return jnp.concatenate([h, l, h], axis=1)

def cat3r(h, l):
    return jnp.concatenate([h, h, l], axis=0)

def compute_kernel(damp_ref, akk_ref, bc_ref, br_ref, a_ref, out_ref, g, yb, w_ref, tl_ref, rh_ref, u_ref):
    i_row = lax.axis_index("row")
    j_col = lax.axis_index("col")
    damp = damp_ref[0:1, :]
    damp2 = jnp.concatenate([damp, damp], axis=1)
    damp4 = jnp.concatenate([damp2, damp2], axis=1)
    g[:, 0:KK] = akk_ref[...]
    g[:, KK:KK + 256] = bc_ref[...]
    posr = lax.broadcasted_iota(jnp.int32, (KK, 512), 0)
    ln = lax.broadcasted_iota(jnp.int32, (KK, 512), 1)
    lm = ln % 256
    posl = jnp.where(lm < 32, (lm // 16) * 512 + (2 * i_row + ln // 256) * 16 + lm % 16, -1)
    g[:, KK + 256:] = br_ref[...] + jnp.where(posr == posl, damp4, 0.0)

    eye = (lax.broadcasted_iota(jnp.int32, (NB, NB), 0) == lax.broadcasted_iota(jnp.int32, (NB, NB), 1))

    def body(b, carry):
        o = pl.multiple_of(b * NB, NB)
        D = g[pl.ds(o, NB), pl.ds(o, NB)] + jnp.where(eye, damp, 0.0)
        w_ref[...] = block_inverse(D)
        for k in range(NBLK):
            @pl.when(b == k)
            def _():
                lo = (k + 1) * NB
                W = w_ref[...]
                wl = cat3l(*split2(W))
                r0 = k * NB
                G = g[r0:r0 + NB, lo:]
                Y = nn(wl, cat3r(*split2(G)))
                g[r0:r0 + NB, lo:] = Y
                if k < NBLK - 1:
                    Mr = KK - lo
                    h, l = split2(Y)
                    lhs = cat3r(h[:, :Mr], l[:, :Mr])
                    lhs = jnp.concatenate([h[:, :Mr], l[:, :Mr], h[:, :Mr]], 0)
                    rhs = cat3r(h, l)
                    tl_ref[:, 0:Mr] = lhs
                    rh_ref[:, 0:KK - lo + LB] = rhs
                    ntile = (KK - lo + LB) // 128
                    def upd(c, _):
                        oo = pl.multiple_of(c * 128, 128)
                        R = tn(tl_ref[:, 0:Mr], rh_ref[:, pl.ds(oo, 128)])
                        gl = pl.ds(pl.multiple_of(oo + lo, 128), 128)
                        g[lo:, gl] = g[lo:, gl] - R
                        return 0
                    lax.fori_loop(0, ntile, upd, 0)
        return carry
    lax.fori_loop(0, NBLK, body, 0)

    U = None
    for t in range(4):
        sl = slice(t * 256, t * 256 + 256)
        rh, rl = split2(g[sl, KK + 256:])
        ch, cl = split2(g[sl, KK:KK + 256])
        P = tn(jnp.concatenate([rh, rl, rh], 0), jnp.concatenate([ch, ch, cl], 0))
        U = P if U is None else U + P
    p0 = g[pl.ds(pl.multiple_of(j_col * 16, 16), 16), KK + 256:]
    p1 = g[pl.ds(pl.multiple_of(512 + j_col * 16, 16), 16), KK + 256:]
    pt = jnp.concatenate([p0, p1, jnp.zeros((96, 512), F32)], 0).T
    r = lax.broadcasted_iota(jnp.int32, (512, 256), 0)
    c = lax.broadcasted_iota(jnp.int32, (512, 256), 1)
    rm = r % 256
    posrow = jnp.where(rm < 32, (rm // 16) * 512 + (2 * i_row + r // 256) * 16 + rm % 16, KK)
    poscol = (c // 16) * 512 + j_col * 16 + c % 16
    A = a_ref[...]
    A = A + jnp.where(r + 512 * i_row == c + 256 * j_col, damp2, 0.0)
    ptw = jnp.concatenate([pt, jnp.zeros((512, 128), F32)], 1)
    out = jnp.where(c >= 32, jnp.where(rm >= 32, A - U, 0.0), jnp.where(posrow >= poscol, ptw, 0.0))
    out_ref[...] = out

def compute(damp, akk, bc, br, a):
    vm = pl.BlockSpec(memory_space=pltpu.VMEM)
    return pl.pallas_call(
        compute_kernel,
        out_shape=jax.ShapeDtypeStruct((512, 256), F32),
        in_specs=[vm] * 5,
        out_specs=vm,
        scratch_shapes=[pltpu.VMEM((KK, KK + LB), F32), pltpu.VMEM((8, 128), F32), pltpu.VMEM((NB, NB), F32),
                        pltpu.VMEM((384, KK - NB), BF16), pltpu.VMEM((384, KK - NB + LB), BF16), pltpu.VMEM((8, 128), F32)],
        compiler_params=pltpu.CompilerParams(vmem_limit_bytes=60 * 1024 * 1024),
        name="eliminate",
    )(damp, akk, bc, br, a)


MESH = pl.DeviceIdType.MESH


def comm_kernel(a_ref, akk, bc, br, damp_ref, zb, tr, bar_unused, zs, zr, zd, xs, xr, ks, kr, kd, us, ur, ds, dr, dd):
    i = lax.axis_index("row")
    j = lax.axis_index("col")
    z = j // 2
    c = lax.rem(j, 2)
    me_partner = (i, 2 * z + 1 - c)

    def zpeer(d):
        return (i, 2 * lax.rem(z + d, 16) + c)

    def xpeer(d):
        return (lax.rem(i + d, 16), j)

    barrier = pltpu.get_barrier_semaphore()

    def greet(d, carry):
        pl.semaphore_signal(barrier, inc=1, device_id=zpeer(d), device_id_type=MESH)
        pl.semaphore_signal(barrier, inc=1, device_id=xpeer(d), device_id_type=MESH)
        return carry

    lax.fori_loop(1, 16, greet, 0)
    pl.semaphore_signal(barrier, inc=1, device_id=me_partner, device_id_type=MESH)

    T = a_ref[:, 0:128].T
    br[0, z, c] = T[0:16, :]
    br[1, z, c] = T[16:32, :]
    lane = lax.broadcasted_iota(jnp.int32, (16, 128), 1)
    x0, y0 = T[0:16, 0:128], T[0:16, 256:384]
    x1, y1 = T[16:32, 0:128], T[16:32, 256:384]
    piece = jnp.where(
        lane < 32,
        x0,
        jnp.where(lane < 64, pltpu.roll(y0, 32, 1), jnp.where(lane < 96, pltpu.roll(x1, 64, 1), pltpu.roll(y1, 96, 1))),
    )
    zb[z, c, 0:16, :] = piece
    r = lax.broadcasted_iota(jnp.int32, (512, 256), 0)
    q = lax.broadcasted_iota(jnp.int32, (512, 256), 1)
    on = r + 512 * i == q + 256 * j
    t = jnp.sum(jnp.where(on, a_ref[...], 0.0), axis=0, keepdims=True)
    t = jnp.sum(t, axis=1, keepdims=True)
    zb[z, c, 16:24, :] = jnp.broadcast_to(t, (8, 128))
    for p in range(2):
        for h in range(2):
            bc[p, i, h] = a_ref[256 * h + 16 * p : 256 * h + 16 * p + 16, :]

    pl.semaphore_wait(barrier, 31)

    def z_send(d):
        return pltpu.make_async_remote_copy(
            src_ref=zb.at[z, c], dst_ref=zb.at[z, c], send_sem=zs.at[d], recv_sem=zr.at[d],
            device_id=zpeer(d), device_id_type=MESH)

    def z_recv(d):
        s = lax.rem(z + 16 - d, 16)
        return pltpu.make_async_remote_copy(
            src_ref=zb.at[s, c], dst_ref=zb.at[s, c], send_sem=zs.at[d], recv_sem=zr.at[d],
            device_id=zpeer(d), device_id_type=MESH)

    def x_send(d):
        return pltpu.make_async_remote_copy(
            src_ref=bc.at[:, i], dst_ref=bc.at[:, i], send_sem=xs.at[d], recv_sem=xr.at[d],
            device_id=xpeer(d), device_id_type=MESH)

    def x_recv(d):
        s = lax.rem(i + 16 - d, 16)
        return pltpu.make_async_remote_copy(
            src_ref=bc.at[:, s], dst_ref=bc.at[:, s], send_sem=xs.at[d], recv_sem=xr.at[d],
            device_id=xpeer(d), device_id_type=MESH)

    up_to = (i, 2 * lax.rem(z + 1, 16) + c)
    down_to = (i, 2 * lax.rem(z + 15, 16) + c)

    def ring(s, up):
        k = lax.rem(z + 16 - s, 16) if up else lax.rem(z + s, 16)
        o = 0 if up else 8
        return pltpu.make_async_remote_copy(
            src_ref=br.at[:, k, c], dst_ref=br.at[:, k, c], send_sem=us.at[s + o], recv_sem=ur.at[s + o],
            device_id=up_to if up else down_to, device_id_type=MESH)

    def ring_in(s, up):
        k = lax.rem(z + 15 - s, 16) if up else lax.rem(z + 1 + s, 16)
        o = 0 if up else 8
        return pltpu.make_async_remote_copy(
            src_ref=br.at[:, k, c], dst_ref=br.at[:, k, c], send_sem=us.at[s + o], recv_sem=ur.at[s + o],
            device_id=up_to if up else down_to, device_id_type=MESH)

    def pair(k):
        return pltpu.make_async_remote_copy(
            src_ref=br.at[:, k, c], dst_ref=br.at[:, k, c], send_sem=ds.at[k], recv_sem=dr.at[k],
            device_id=me_partner, device_id_type=MESH)

    def pair_in(k):
        return pltpu.make_async_remote_copy(
            src_ref=br.at[:, k, 1 - c], dst_ref=br.at[:, k, 1 - c], send_sem=ds.at[k], recv_sem=dr.at[k],
            device_id=me_partner, device_id_type=MESH)

    def go(f):
        def step(d, carry):
            f(d)
            return carry
        return step

    lax.fori_loop(1, 16, go(lambda d: z_send(d).start()), 0)
    ring(0, True).start()
    ring(0, False).start()
    pair(z).start()
    lax.fori_loop(1, 16, go(lambda d: x_send(d).start()), 0)

    def ring_step(s, last=False):
        ring_in(s - 1, True).wait_recv()
        ring(s, True).start()
        pair(lax.rem(z + 16 - s, 16)).start()
        ring_in(s - 1, False).wait_recv()
        if not last:
            ring(s, False).start()
        pair(lax.rem(z + s, 16)).start()

    for s in (1, 2):
        ring_step(s)

    lax.fori_loop(1, 16, go(lambda d: z_recv(d).wait_recv()), 0)
    zpair = pltpu.make_async_remote_copy(
        src_ref=zb.at[:, c], dst_ref=zb.at[:, c], send_sem=zd.at[0], recv_sem=zd.at[1],
        device_id=me_partner, device_id_type=MESH)
    zpair.start()
    pltpu.make_async_remote_copy(
        src_ref=zb.at[:, 1 - c], dst_ref=zb.at[:, 1 - c], send_sem=zd.at[0], recv_sem=zd.at[1],
        device_id=me_partner, device_id_type=MESH).wait_recv()
    G = zb[:, :, 0:16, :].reshape(512, 128).T
    rowsum = jnp.sum(zb[:, :, 16:24, :].reshape(32, 8, 128), axis=0)
    tr[i] = rowsum
    akk[0, i, c, :, 0:512] = jnp.where(c == 0, G[0:16, :], G[32:48, :])
    akk[0, i, c, :, 512:1024] = jnp.where(c == 0, G[64:80, :], G[96:112, :])
    akk[1, i, c, :, 512:1024] = jnp.where(c == 0, G[80:96, :], G[112:128, :])

    def k_copy(d, s, n):
        src = (akk.at[0, s, c], akk.at[1, s, c, :, pl.ds(512, 512)], tr.at[s])[n]
        return pltpu.make_async_remote_copy(
            src_ref=src, dst_ref=src, send_sem=ks.at[n, d], recv_sem=kr.at[n, d],
            device_id=xpeer(d), device_id_type=MESH)

    for n in range(3):
        lax.fori_loop(1, 16, go(lambda d: k_copy(d, i, n).start()), 0)
    for s in range(3, 7):
        ring_step(s)
    ring_step(7, last=True)

    for n in range(3):
        lax.fori_loop(1, 16, go(lambda d: k_copy(d, lax.rem(i + 16 - d, 16), n).wait_recv()), 0)

    def kpair(n, h):
        src = (akk.at[0, :, h], akk.at[1, :, h, :, pl.ds(512, 512)])[n]
        return pltpu.make_async_remote_copy(
            src_ref=src, dst_ref=src, send_sem=kd.at[n], recv_sem=kd.at[2 + n],
            device_id=me_partner, device_id_type=MESH)

    kpair(0, c).start()
    kpair(1, c).start()
    damp_ref[...] = jnp.sum(tr[...], axis=0) * (damping_share / 8192.0)

    ring_in(7, True).wait_recv()
    pair(lax.rem(z + 8, 16)).start()
    lax.fori_loop(1, 16, go(lambda d: x_recv(d).wait_recv()), 0)
    lax.fori_loop(0, 16, go(lambda k: pair_in(k).wait_recv()), 0)
    kpair(0, 1 - c).wait_recv()
    kpair(1, 1 - c).wait_recv()

    lax.fori_loop(1, 16, go(lambda d: z_send(d).wait_send()), 0)
    lax.fori_loop(1, 16, go(lambda d: x_send(d).wait_send()), 0)
    for n in range(3):
        lax.fori_loop(1, 16, go(lambda d: k_copy(d, i, n).wait_send()), 0)
    for s in range(8):
        ring(s, True).wait_send()
        if s < 7:
            ring(s, False).wait_send()
    lax.fori_loop(0, 16, go(lambda k: pair(k).wait_send()), 0)
    zpair.wait_send()
    kpair(0, c).wait_send()
    kpair(1, c).wait_send()


def gather(a):
    vm = pl.BlockSpec(memory_space=pltpu.VMEM)
    dma = pltpu.SemaphoreType.DMA
    return pl.pallas_call(
        comm_kernel,
        out_shape=[
            jax.ShapeDtypeStruct((2, 16, 2, 16, 1024), F32),
            jax.ShapeDtypeStruct((2, 16, 2, 16, 256), F32),
            jax.ShapeDtypeStruct((2, 16, 2, 16, 512), F32),
            jax.ShapeDtypeStruct((8, 128), F32),
        ],
        in_specs=[vm],
        out_specs=[vm] * 4,
        scratch_shapes=[
            pltpu.VMEM((16, 2, 24, 128), F32), pltpu.VMEM((16, 8, 128), F32), pltpu.VMEM((8, 128), F32),
            dma((16,)), dma((16,)), dma((2,)), dma((16,)), dma((16,)), dma((3, 16)), dma((3, 16)), dma((4,)),
            dma((16,)), dma((16,)), dma((16,)), dma((16,)), dma((1,)),
        ],
        compiler_params=pltpu.CompilerParams(collective_id=0, has_side_effects=True, vmem_limit_bytes=32 * 1024 * 1024),
        name="gather",
    )(a)


def on_device(factors):
    a = factors[0]
    akk, bc, br, damp = gather(a)
    out = compute(damp, akk.reshape(1024, 1024), bc.reshape(1024, 256), br.reshape(1024, 512), a)
    return out[None]


def solution(mesh):
    placed = P(None, "row", "col")
    return jax.shard_map(on_device, mesh=mesh, in_specs=(placed,), out_specs=placed, check_vma=False)
```

time: 514 us -> 128 us (0.25)
  other arithmetic: 246 us -> 0 us
  Pallas kernels: 0 us -> 121 us
  blocking collectives: 109 us -> 0 us
  matrix products: 39.1 us -> 0 us
  local copies, waits for them, and re-layouts: 44.1 us -> 5.87 us
  starting transfers between devices: 34.2 us -> 0 us
  waiting for transfers between devices: 29.8 us -> 0 us
  between operations: 6.76 us -> 0.02 us
    another operation x34 -> x0, other arithmetic: 240 us -> none  [the longest x29 158 us: on_device(): factor_kk = jnp.linalg.cholesky(diag_block)]
    pallas_call x0 -> x2, Pallas kernels: none -> 121 us  [the longest x1 62.8 us: gather(): pl.pallas_call(comm_kernel, out_shape=[jax.ShapeDtypeStruct((2, 16, 2, 16...]
    psum x4 -> x0, blocking collectives: 63.8 us -> none  [one_axis_at_a_time(): x = lax.psum(x, axis)]
    all_to_all x2 -> x0, blocking collectives: 45 us -> none  [from_everyone(): return lax.all_to_all(copies, axis, split_axis=0, concat_axis=0, tiled=True)]
    all_to_all x6 -> x0, starting transfers between devices: 34.2 us -> none  [from_everyone(): return lax.all_to_all(copies, axis, split_axis=0, concat_axis=0, tiled=True)]
    all_to_all x6 -> x0, waiting for transfers between devices: 29.8 us -> none  [from_everyone(): return lax.all_to_all(copies, axis, split_axis=0, concat_axis=0, tiled=True)]
    another operation x45 -> x0, local copies, waits for them, and re-layouts: 26.9 us -> none  [the longest x27 23.5 us: on_device(): jax.scipy.linalg.solve_triangular(factor_kk, identity, lower=True)]
    another operation x26 -> x0, matrix products: 23 us -> none  [the longest x14 11.5 us: on_device(): jax.scipy.linalg.solve_triangular(factor_kk, identity, lower=True)]
  transfers between devices with their start and end apart: 6 -> 0, of which waited for: 2 -> 0; matrix products, arithmetic and copies ran while one was open for 59% -> 0% of each run, Pallas kernels for 0% -> 0%
where the time goes in v1:
time: 128 us; the launch traced here: 127 us
  Pallas kernels  121 us (95%)
  local copies, waits for them, and re-layouts  5.87 us (5%)
    pallas_call x1, Pallas kernels, gather(): pl.pallas_call(comm_kernel, out_shape=[jax.ShapeDtypeStruct((2, 16, 2, 16...  62.8 us
    pallas_call x1, Pallas kernels, compute(): pl.pallas_call(compute_kernel, out_shape=jax.ShapeDtypeStruct((512, 256),...  58.7 us
    unnamed x10, local copies, waits for them, and re-layouts  5.87 us

profile of v1, /device:TPU:1, one launch (start us, length us, event | category | flops | bytes accessed | tf_op | source)
XLA Modules:
  0.0 127.4 jit_solution(17618289556421280501)
XLA Ops:
  0.0 0.0 copy-start.2
  0.0 1.0 copy-done.2
  1.0 62.8 %gather.1 = (f32[2,16,2,16,1024]{4,3,2,1,0:T(8,128)S(1)}, f32[2,16,2,16,256]{4,3,2,1,0:T(8,128)S(1)}, f32[2,16,2,16,512]{4,3,2,1,0:T(8,128)S(1)}, f32[8,128]{1,0:T(8,128)S(1)}) custom-call(f32[512,256]{1,0:T(8,128)S(1)} %bitcast.8), custom_call_target="tpu_custom_call" | custom-call | tf_op jit(solution)/shard_map/gather/pallas_call | solution.py:357
  63.8 0.0 copy-start
  63.8 1.9 %copy-done = f32[2,16,2,16,1024]{4,3,2,1,0:T(8,128)} copy-done((f32[2,16,2,16,1024]{4,3,2,1,0:T(8,128)}, f32[2,16,2,16,1024]{4,3,2,1,0:T(8,128)S(1)}, u32[]{:S(2)}) %copy-start) | copy-done | bytes 4194328
  65.8 0.0 copy-start.1
  65.8 1.3 %copy-done.1 = f32[2,16,2,16,512]{4,3,2,1,0:T(8,128)} copy-done((f32[2,16,2,16,512]{4,3,2,1,0:T(8,128)}, f32[2,16,2,16,512]{4,3,2,1,0:T(8,128)S(1)}, u32[]{:S(2)}) %copy-start.1) | copy-done | bytes 2097176
  67.1 0.0 copy-start.3
  67.1 1.0 copy-done.3
  68.1 0.0 copy-start.4
  68.1 0.6 copy-done.4
  68.7 58.7 %eliminate.1 = f32[512,256]{1,0:T(8,128)} custom-call(f32[8,128]{1,0:T(8,128)} %copy-done.4, f32[1024,1024]{1,0:T(8,128)} %bitcast.5, f32[1024,256]{1,0:T(8,128)} %bitcast.9, f32[1024,512]{1,0:T(8,128)} %bitcast.6, f32[512,256]{1,0:T(8,128)} %bitcast.7), custom_call_target="tpu_custom_call" | custom-call | tf_op jit(solution)/shard_map/eliminate/pallas_call | solution.py:158
Async XLA Ops:
  0.0 1.0 copy-start.2
  63.8 1.9 %copy-start = (f32[2,16,2,16,1024]{4,3,2,1,0:T(8,128)}, f32[2,16,2,16,1024]{4,3,2,1,0:T(8,128)S(1)}, u32[]{:S(2)}) copy-start(f32[2,16,2,16,1024]{4,3,2,1,0:T(8,128)S(1)} %get-tuple-element.10) | copy-start | bytes 12582916
  65.8 1.3 %copy-start.1 = (f32[2,16,2,16,512]{4,3,2,1,0:T(8,128)}, f32[2,16,2,16,512]{4,3,2,1,0:T(8,128)S(1)}, u32[]{:S(2)}) copy-start(f32[2,16,2,16,512]{4,3,2,1,0:T(8,128)S(1)} %get-tuple-element.12) | copy-start | bytes 6291460
  67.1 1.0 copy-start.3
  68.1 0.6 copy-start.4

commit v2 on v0

v2 whole, which is shorter than its diff:
```python
import jax
import jax.numpy as jnp
from jax import lax
from jax.experimental import pallas as pl
from jax.experimental.pallas import tpu as pltpu
from jax.sharding import PartitionSpec as P

F32, BF16 = jnp.float32, jnp.bfloat16
MESH = pl.DeviceIdType.MESH
damping_share = 0.03162277660168379
NB = 128
MINI = 32
PS = 512
RW = PS + 256 + 512


def split3(x):
    h = x.astype(BF16)
    r = x - h.astype(F32)
    m = r.astype(BF16)
    return h, m, (r - m.astype(F32)).astype(BF16)


def split2(x):
    h = x.astype(BF16)
    return h, (x - h.astype(F32)).astype(BF16)


def tn(a, b):
    return lax.dot_general(a, b, (((0,), (0,)), ((), ())), preferred_element_type=F32)


def nn(a, b):
    return lax.dot_general(a, b, (((1,), (0,)), ((), ())), preferred_element_type=F32)


def left3(h, l):
    return jnp.concatenate([h, l, h], axis=1)


def right3(h, l):
    return jnp.concatenate([h, h, l], axis=0)


def block_inverse(M, b=MINI):
    n = 128
    H = b // 8
    sub = lax.broadcasted_iota(jnp.int32, (8, n), 0)
    lane = lax.broadcasted_iota(jnp.int32, (8, n), 1)
    M = [M[8 * i:8 * i + 8, :] for i in range(n // 8)]
    for s in range(n // b):
        r0 = s * b
        q0 = r0 // 8
        S = [[None] * b for _ in range(H)]
        for k in range(b):
            for h in range(k // 8, H):
                S[h][k] = jnp.broadcast_to(M[q0 + h][:, r0 + k:r0 + k + 1], (8, n))
        inblk = (lane >= r0) & (lane < r0 + b)
        N = [jnp.where(inblk, jnp.where(lane - r0 == sub + 8 * h, 1.0, 0.0).astype(F32), M[q0 + h]) for h in range(H)]
        scale = [None] * H
        for j in range(b):
            hj, sj = j // 8, j % 8
            piv = jnp.broadcast_to(S[hj][j][sj:sj + 1, :], (8, n))
            rs = lax.rsqrt(piv)
            rinv = rs * rs
            scale[hj] = rs if sj == 0 else jnp.where(sub == sj, rs, scale[hj])
            if j == b - 1:
                break
            for k in range(j + 1, b):
                hk, sk = k // 8, k % 8
                t = jnp.broadcast_to(S[hk][j][sk:sk + 1, :], (8, n)) * rinv
                for h in range(hk, H):
                    S[h][k] = S[h][k] - S[h][j] * t
            prow = jnp.broadcast_to(N[hj][sj:sj + 1, :], (8, n)) * rinv
            for h in range(hj, H):
                if h == hj:
                    if sj == 7:
                        continue
                    N[h] = jnp.where(sub > sj, N[h] - S[h][j] * prow, N[h])
                else:
                    N[h] = N[h] - S[h][j] * prow
        Y = jnp.concatenate([N[h] * scale[h] for h in range(H)], axis=0)
        lb = lax.broadcasted_iota(jnp.int32, (b, n), 1)
        for h in range(H):
            M[q0 + h] = Y[8 * h:8 * h + 8, :] if s == n // b - 1 else jnp.where(lane < r0 + b, Y[8 * h:8 * h + 8, :], 0.0)
        if s < n // b - 1:
            h_, m_, l_ = split3(Y)
            R = tn(jnp.concatenate([h_, h_, m_, h_, l_, m_], 0), jnp.concatenate([h_, m_, h_, l_, h_, m_], 0))
            for q in range(q0 + H, n // 8):
                M[q] = jnp.where(inblk, 0.0, M[q]) - R[8 * q:8 * q + 8, :]
    return jnp.concatenate(M, axis=0)

def kernel(a_ref, out_ref, akk, bc, br, zb, tz, tx, dn, wst, lh, ll, kh, kl, g0, g1, ph, pm, qh, ql, y0, y1, w_ref,
           zs, zr, zd, ts, tr, xs, xr, ks, kr, kd, hs, hr, us, ur, ds, dr):
    i = lax.axis_index("row")
    j = lax.axis_index("col")
    z = j // 2
    c = lax.rem(j, 2)
    partner = (i, 2 * z + 1 - c)

    def zpeer(d):
        return (i, 2 * lax.rem(z + d, 16) + c)

    def xpeer(d):
        return (lax.rem(i + d, 16), j)

    def copy(src, dst, ssem, rsem, dev):
        return pltpu.make_async_remote_copy(
            src_ref=src, dst_ref=dst, send_sem=ssem, recv_sem=rsem, device_id=dev, device_id_type=MESH)

    def each(lo, hi, f):
        def step(d, carry):
            f(d)
            return carry
        lax.fori_loop(lo, hi, step, 0)

    barrier = pltpu.get_barrier_semaphore()

    def greet(d):
        pl.semaphore_signal(barrier, inc=1, device_id=zpeer(d), device_id_type=MESH)
        pl.semaphore_signal(barrier, inc=1, device_id=xpeer(d), device_id_type=MESH)

    each(1, 16, greet)
    pl.semaphore_signal(barrier, inc=1, device_id=partner, device_id_type=MESH)

    T = a_ref[:, 0:128].T
    br[0, z, c] = T[0:16, :]
    br[1, z, c] = T[16:32, :]
    lane = lax.broadcasted_iota(jnp.int32, (16, 128), 1)
    p0, p1 = T[0:16, 0:128], T[0:16, 256:384]
    p2, p3 = T[16:32, 0:128], T[16:32, 256:384]
    zb[z, c] = jnp.where(
        lane < 32, p0,
        jnp.where(lane < 64, pltpu.roll(p1, 32, 1), jnp.where(lane < 96, pltpu.roll(p2, 64, 1), pltpu.roll(p3, 96, 1))))
    r = lax.broadcasted_iota(jnp.int32, (512, 256), 0)
    q = lax.broadcasted_iota(jnp.int32, (512, 256), 1)
    on_diagonal = r + 512 * i == q + 256 * j
    t = jnp.sum(jnp.where(on_diagonal, a_ref[...], 0.0), axis=0, keepdims=True)
    tz[z, c] = jnp.broadcast_to(jnp.sum(t, axis=1, keepdims=True), (1, 128))
    for p in range(2):
        for h in range(2):
            bc[p, i, h] = a_ref[256 * h + 16 * p : 256 * h + 16 * p + 16, :]

    pl.semaphore_wait(barrier, 31)

    def behind(v, d):
        return lax.rem(v + 16 - d, 16)

    def z_copy(d, s):
        return copy(zb.at[s, c], zb.at[s, c], zs.at[d], zr.at[d], zpeer(d))

    def t_copy(d, s):
        return copy(tz.at[s, c], tz.at[s, c], ts.at[d], tr.at[d], zpeer(d))

    def x_copy(d, s):
        return copy(bc.at[:, s], bc.at[:, s], xs.at[d], xr.at[d], xpeer(d))

    def h_copy(d, s):
        return copy(tx.at[s], tx.at[s], hs.at[d], hr.at[d], xpeer(d))

    def strip(n, s, h):
        return (akk.at[0, s, h, :, pl.ds(0, 512)], akk.at[0, s, h, :, pl.ds(512, 512)],
                akk.at[1, s, h, :, pl.ds(512, 512)])[n]

    def k_copy(n, d, s):
        return copy(strip(n, s, c), strip(n, s, c), ks.at[n, d], kr.at[n, d], xpeer(d))

    def k_pair(n, h):
        v = (akk.at[0, :, h, :, pl.ds(0, 512)], akk.at[0, :, h, :, pl.ds(512, 512)],
             akk.at[1, :, h, :, pl.ds(512, 512)])[n]
        return copy(v, v, kd.at[n], kd.at[3 + n], partner)

    def z_pair(h):
        return copy(zb.at[:, h], zb.at[:, h], zd.at[0], zd.at[1], partner)

    def t_pair(h):
        return copy(tz.at[:, h], tz.at[:, h], zd.at[2], zd.at[3], partner)

    up_to = (i, 2 * lax.rem(z + 1, 16) + c)
    down_to = (i, 2 * lax.rem(z + 15, 16) + c)

    def ring(s, up, arriving=False):
        e = s + 1 if arriving else s
        k = behind(z, e) if up else lax.rem(z + e, 16)
        o = 0 if up else 8
        return copy(br.at[:, k, c], br.at[:, k, c], us.at[s + o], ur.at[s + o], up_to if up else down_to)

    def pair(k, h):
        return copy(br.at[:, k, h], br.at[:, k, h], ds.at[k], dr.at[k], partner)

    def ring_step(s):
        ring(s - 1, True, True).wait_recv()
        ring(s, True).start()
        pair(behind(z, s), c).start()
        ring(s - 1, False, True).wait_recv()
        if s < 7:
            ring(s, False).start()
        pair(lax.rem(z + s, 16), c).start()

    each(1, 16, lambda d: z_copy(d, z).start())
    each(1, 16, lambda d: t_copy(d, z).start())
    ring(0, True).start()
    ring(0, False).start()
    pair(z, c).start()

    each(1, 16, lambda d: t_copy(d, behind(z, d)).wait_recv())
    t_pair(c).start()
    each(1, 16, lambda d: z_copy(d, behind(z, d)).wait_recv())
    z_pair(c).start()
    t_pair(1 - c).wait_recv()
    tx[i] = jnp.sum(tz[...].reshape(32, 1, 128), axis=0)
    each(1, 16, lambda d: h_copy(d, i).start())
    z_pair(1 - c).wait_recv()
    S = zb[...].reshape(512, 128).T
    akk[0, i, c, :, 0:512] = jnp.where(c == 0, S[0:16, :], S[32:48, :])
    akk[0, i, c, :, 512:1024] = jnp.where(c == 0, S[64:80, :], S[96:112, :])
    akk[1, i, c, :, 512:1024] = jnp.where(c == 0, S[80:96, :], S[112:128, :])
    each(1, 16, lambda d: k_copy(0, d, i).start())
    each(1, 16, lambda d: k_copy(1, d, i).start())
    each(1, 16, lambda d: x_copy(d, i).start())
    each(1, 16, lambda d: k_copy(2, d, i).start())
    ring_step(1)
    ring_step(2)
    each(1, 16, lambda d: h_copy(d, behind(i, d)).wait_recv())
    damp = jnp.sum(tx[...], axis=0) * (damping_share / 8192.0)
    each(1, 16, lambda d: k_copy(0, d, behind(i, d)).wait_recv())
    k_pair(0, c).start()
    ring_step(3)
    k_pair(0, 1 - c).wait_recv()

    damp2 = jnp.concatenate([damp, damp], axis=1)
    damp4 = jnp.concatenate([damp2, damp2], axis=1)
    eye = lax.broadcasted_iota(jnp.int32, (NB, NB), 0) == lax.broadcasted_iota(jnp.int32, (NB, NB), 1)
    deye = jnp.where(eye, damp, 0.0)
    ln = lax.broadcasted_iota(jnp.int32, (PS, 512), 1)
    posl = jnp.where(ln % 256 < 32, (ln % 256 // 16) * 512 + (2 * i + ln // 256) * 16 + ln % 16, -1)
    posr = lax.broadcasted_iota(jnp.int32, (PS, 512), 0)

    g0[...] = akk[0, :, :, :, 0:512].reshape(512, 512)
    dn[...] = g0[0:NB, 0:NB]

    def middle():
        ring(7, True, True).wait_recv()
        pair(lax.rem(z + 8, 16), c).start()
        each(1, 16, lambda d: k_copy(1, d, behind(i, d)).wait_recv())
        k_pair(1, c).start()
        each(1, 16, lambda d: x_copy(d, behind(i, d)).wait_recv())
        each(1, 16, lambda d: k_copy(2, d, behind(i, d)).wait_recv())
        k_pair(2, c).start()
        each(0, 16, lambda k: pair(k, 1 - c).wait_recv())
        k_pair(1, 1 - c).wait_recv()
        k_pair(2, 1 - c).wait_recv()
        for b in range(4):
            o = b * NB
            rows = slice(o, o + NB)
            acc = jnp.concatenate([
                akk[0, 4 * b : 4 * b + 4, :, :, 512:1024].reshape(NB, 512),
                bc[0, 4 * b : 4 * b + 4].reshape(NB, 256),
                br[0, 4 * b : 4 * b + 4].reshape(NB, 512) + jnp.where(posr[rows] == posl[rows], damp4, 0.0)], axis=1)
            if b:
                acc = acc - nn(
                    jnp.concatenate([lh[rows, 0:o], ll[rows, 0:o], lh[rows, 0:o]], axis=1),
                    jnp.concatenate([ph[0:o, :], ph[0:o, :], pm[0:o, :]], axis=0))
            Y = nn(wst[b], right3(*split2(acc)))
            y0[rows, :] = Y[:, PS + 256 :]
            ph[rows, :], pm[rows, :] = split2(Y)
            th, tl = split2(Y[:, 0:PS].T)
            kh[:, o : o + NB] = th
            kl[:, o : o + NB] = tl
        left = jnp.concatenate([kh[...], kl[...], kh[...]], axis=1)
        for o in range(0, RW, 256):
            R = nn(left, jnp.concatenate([ph[:, o : o + 256], ph[:, o : o + 256], pm[:, o : o + 256]], axis=0))
            if o < PS:
                src = akk[1, :, :, :, 512 + o : 768 + o].reshape(512, 256)
            elif o == PS:
                src = bc[1].reshape(512, 256)
            else:
                v = o - PS - 256
                src = br[1, :, :, :, v : v + 256].reshape(512, 256) + jnp.where(
                    posr[:, v : v + 256] + 512 == posl[:, v : v + 256], damp2, 0.0)
            g1[:, o : o + 256] = src - R
        dn[...] = g1[0:NB, 0:NB]

    def body(b, carry):
        w_ref[...] = block_inverse(dn[...] + deye)
        for k in range(8):

            @pl.when(b == k)
            def _():
                wl = left3(*split2(w_ref[...]))
                kk = k % 4
                lo = (kk + 1) * NB
                rows = slice(kk * NB, lo)
                if k < 4:
                    wst[k] = wl
                    ring_step(4 + k)
                    if k == 3:
                        middle()
                        return
                    g, hi = g0, PS
                else:
                    g, hi = g1, RW
                Y = nn(wl, right3(*split2(g[rows, lo:hi])))
                h, l = split2(Y)
                if k >= 4:
                    y1[rows, :] = Y[:, PS + 256 - lo :]
                    qh[rows, :] = h[:, PS - lo :]
                    ql[rows, :] = l[:, PS - lo :]
                if kk < 3:
                    th, tl = split2(Y[:, 0 : PS - lo].T)
                    if k < 4:
                        lh[lo:PS, rows] = th
                        ll[lo:PS, rows] = tl
                    left = left3(th, tl)
                    right = right3(h, l)
                    for o in range(0, hi - lo, 256):
                        e = min(o + 256, hi - lo)
                        g[lo:PS, lo + o : lo + e] = g[lo:PS, lo + o : lo + e] - nn(left, right[:, o:e])
                    dn[...] = g[lo : lo + NB, lo : lo + NB]
        return carry

    lax.fori_loop(0, 8, body, 0)

    U = None
    for yh, yl, base in ((ph, pm, PS), (qh, ql, 0)):
        for o in (0, 256):
            s = slice(o, o + 256)
            rh, rl = yh[s, base + 256 :], yl[s, base + 256 :]
            ch, cl = yh[s, base : base + 256], yl[s, base : base + 256]
            X = tn(jnp.concatenate([rh, rl, rh], 0), jnp.concatenate([ch, ch, cl], 0))
            U = X if U is None else U + X
    at = pl.ds(pl.multiple_of(j * 16, 16), 16)
    cols = jnp.concatenate([y0[at, :], y1[at, :], jnp.zeros((96, 512), F32)], 0).T
    rm = r % 256
    posrow = jnp.where(rm < 32, (rm // 16) * 512 + (2 * i + r // 256) * 16 + rm % 16, 1024)
    poscol = (q // 16) * 512 + j * 16 + q % 16
    A = a_ref[...] + jnp.where(on_diagonal, damp2, 0.0)
    cols = jnp.concatenate([cols, jnp.zeros((512, 128), F32)], 1)
    out_ref[...] = jnp.where(
        q >= 32, jnp.where(rm >= 32, A - U, 0.0), jnp.where(posrow >= poscol, cols, 0.0))

    each(1, 16, lambda d: z_copy(d, z).wait_send())
    each(1, 16, lambda d: t_copy(d, z).wait_send())
    each(1, 16, lambda d: x_copy(d, i).wait_send())
    each(1, 16, lambda d: h_copy(d, i).wait_send())
    for n in range(3):
        each(1, 16, lambda d: k_copy(n, d, i).wait_send())
        k_pair(n, c).wait_send()
    for s in range(8):
        ring(s, True).wait_send()
        if s < 7:
            ring(s, False).wait_send()
    each(0, 16, lambda k: pair(k, c).wait_send())
    z_pair(c).wait_send()
    t_pair(c).wait_send()


def on_device(factors):
    vm = pl.BlockSpec(memory_space=pltpu.VMEM)
    dma = pltpu.SemaphoreType.DMA
    v = pltpu.VMEM
    out = pl.pallas_call(
        kernel,
        out_shape=jax.ShapeDtypeStruct((512, 256), F32),
        in_specs=[vm],
        out_specs=vm,
        scratch_shapes=[
            v((2, 16, 2, 16, 1024), F32), v((2, 16, 2, 16, 256), F32), v((2, 16, 2, 16, 512), F32),
            v((16, 2, 16, 128), F32), v((16, 2, 1, 128), F32), v((16, 1, 128), F32),
            v((NB, NB), F32), v((4, NB, 3 * NB), BF16), v((PS, PS), BF16), v((PS, PS), BF16), v((PS, PS), BF16), v((PS, PS), BF16),
            v((PS, PS), F32), v((PS, RW), F32), v((PS, RW), BF16), v((PS, RW), BF16),
            v((PS, 768), BF16), v((PS, 768), BF16), v((PS, 512), F32), v((PS, 512), F32), v((NB, NB), F32),
            dma((16,)), dma((16,)), dma((4,)), dma((16,)), dma((16,)), dma((16,)), dma((16,)),
            dma((3, 16)), dma((3, 16)), dma((6,)), dma((16,)), dma((16,)), dma((16,)), dma((16,)),
            dma((16,)), dma((16,)),
        ],
        compiler_params=pltpu.CompilerParams(
            collective_id=0, has_side_effects=True, vmem_limit_bytes=56 * 1024 * 1024),
        name="refresh",
    )(factors[0])
    return out[None]


def solution(mesh):
    placed = P(None, "row", "col")
    return jax.shard_map(on_device, mesh=mesh, in_specs=(placed,), out_specs=placed, check_vma=False)
```

time: 514 us -> 103 us (0.20)
  the two profiles are of different devices: /device:TPU:1 before, /device:TPU:7 now
where the time goes in v2:
time: 103 us; the launch traced here: 102 us
  Pallas kernels  100 us (97%)
  local copies, waits for them, and re-layouts  1.87 us (2%)
    pallas_call x1, Pallas kernels, on_device(): pl.pallas_call(kernel, out_shape=jax.ShapeDtypeStruct((512, 256), F32), i...  100 us

profile of v2, /device:TPU:7, one launch (start us, length us, event | category | flops | bytes accessed | tf_op | source)
XLA Modules:
  0.0 102.3 jit_solution(2547883124795600922)
XLA Ops:
  0.0 100.5 %refresh.1 = f32[512,256]{1,0:T(8,128)} custom-call(f32[512,256]{1,0:T(8,128)} %bitcast.3), custom_call_target="tpu_custom_call" | custom-call | tf_op jit(solution)/shard_map/refresh/pallas_call | solution.py:362
  100.5 1.9 %copy.3 = f32[1,512,256]{2,1,0:T(8,128)} copy(f32[1,512,256]{2,1,0:T(8,128)} %bitcast.2) | data formatting | bytes 1048576

commit v3 on v2

--- a/solution.py
+++ b/solution.py
@@ -58,27 +58,29 @@
         inblk = (lane >= r0) & (lane < r0 + b)
         N = [jnp.where(inblk, jnp.where(lane - r0 == sub + 8 * h, 1.0, 0.0).astype(F32), M[q0 + h]) for h in range(H)]
         scale = [None] * H
+        d = jnp.broadcast_to(S[0][0][0:1, :], (8, n))
         for j in range(b):
             hj, sj = j // 8, j % 8
-            piv = jnp.broadcast_to(S[hj][j][sj:sj + 1, :], (8, n))
-            rs = lax.rsqrt(piv)
-            rinv = rs * rs
+            rs = lax.rsqrt(d)
             scale[hj] = rs if sj == 0 else jnp.where(sub == sj, rs, scale[hj])
             if j == b - 1:
                 break
+            row = [None] * b
             for k in range(j + 1, b):
-                hk, sk = k // 8, k % 8
-                t = jnp.broadcast_to(S[hk][j][sk:sk + 1, :], (8, n)) * rinv
-                for h in range(hk, H):
-                    S[h][k] = S[h][k] - S[h][j] * t
-            prow = jnp.broadcast_to(N[hj][sj:sj + 1, :], (8, n)) * rinv
+                row[k] = jnp.broadcast_to(S[k // 8][j][k % 8 : k % 8 + 1, :], (8, n))
+            rinv = rs * rs
+            hn, sn = (j + 1) // 8, (j + 1) % 8
+            d = jnp.broadcast_to(S[hn][j + 1][sn : sn + 1, :], (8, n)) - (row[j + 1] * row[j + 1]) * rinv
+            u = [S[h][j] * rinv if h >= hj else None for h in range(H)]
+            for k in range(j + 1, b):
+                for h in range(k // 8, H):
+                    S[h][k] = S[h][k] - u[h] * row[k]
+            prow = jnp.broadcast_to(N[hj][sj : sj + 1, :], (8, n))
             for h in range(hj, H):
-                if h == hj:
-                    if sj == 7:
-                        continue
-                    N[h] = jnp.where(sub > sj, N[h] - S[h][j] * prow, N[h])
-                else:
-                    N[h] = N[h] - S[h][j] * prow
+                if h > hj:
+                    N[h] = N[h] - u[h] * prow
+                elif sj < 7:
+                    N[h] = N[h] - jnp.where(sub > sj, u[h], 0.0) * prow
         Y = jnp.concatenate([N[h] * scale[h] for h in range(H)], axis=0)
         lb = lax.broadcasted_iota(jnp.int32, (b, n), 1)
         for h in range(H):
@@ -202,30 +204,31 @@
     ring(0, True).start()
     ring(0, False).start()
     pair(z, c).start()
-
+    each(1, 16, lambda d: x_copy(d, i).start())
+    ring_step(1)
+    ring_step(2)
     each(1, 16, lambda d: t_copy(d, behind(z, d)).wait_recv())
     t_pair(c).start()
     each(1, 16, lambda d: z_copy(d, behind(z, d)).wait_recv())
     z_pair(c).start()
+    ring_step(3)
     t_pair(1 - c).wait_recv()
     tx[i] = jnp.sum(tz[...].reshape(32, 1, 128), axis=0)
     each(1, 16, lambda d: h_copy(d, i).start())
     z_pair(1 - c).wait_recv()
     S = zb[...].reshape(512, 128).T
     akk[0, i, c, :, 0:512] = jnp.where(c == 0, S[0:16, :], S[32:48, :])
+    each(1, 16, lambda d: k_copy(0, d, i).start())
     akk[0, i, c, :, 512:1024] = jnp.where(c == 0, S[64:80, :], S[96:112, :])
     akk[1, i, c, :, 512:1024] = jnp.where(c == 0, S[80:96, :], S[112:128, :])
-    each(1, 16, lambda d: k_copy(0, d, i).start())
-    each(1, 16, lambda d: k_copy(1, d, i).start())
-    each(1, 16, lambda d: x_copy(d, i).start())
-    each(1, 16, lambda d: k_copy(2, d, i).start())
-    ring_step(1)
-    ring_step(2)
+    ring_step(4)
     each(1, 16, lambda d: h_copy(d, behind(i, d)).wait_recv())
     damp = jnp.sum(tx[...], axis=0) * (damping_share / 8192.0)
+    ring_step(5)
     each(1, 16, lambda d: k_copy(0, d, behind(i, d)).wait_recv())
     k_pair(0, c).start()
-    ring_step(3)
+    each(1, 16, lambda d: k_copy(1, d, i).start())
+    each(1, 16, lambda d: k_copy(2, d, i).start())
     k_pair(0, 1 - c).wait_recv()
 
     damp2 = jnp.concatenate([damp, damp], axis=1)
@@ -240,8 +243,6 @@
     dn[...] = g0[0:NB, 0:NB]
 
     def middle():
-        ring(7, True, True).wait_recv()
-        pair(lax.rem(z + 8, 16), c).start()
         each(1, 16, lambda d: k_copy(1, d, behind(i, d)).wait_recv())
         k_pair(1, c).start()
         each(1, 16, lambda d: x_copy(d, behind(i, d)).wait_recv())
@@ -293,7 +294,11 @@
                 rows = slice(kk * NB, lo)
                 if k < 4:
                     wst[k] = wl
-                    ring_step(4 + k)
+                    if k < 2:
+                        ring_step(6 + k)
+                    if k == 2:
+                        ring(7, True, True).wait_recv()
+                        pair(lax.rem(z + 8, 16), c).start()
                     if k == 3:
                         middle()
                         return
@@ -321,14 +326,10 @@
 
     lax.fori_loop(0, 8, body, 0)
 
-    U = None
-    for yh, yl, base in ((ph, pm, PS), (qh, ql, 0)):
-        for o in (0, 256):
-            s = slice(o, o + 256)
-            rh, rl = yh[s, base + 256 :], yl[s, base + 256 :]
-            ch, cl = yh[s, base : base + 256], yl[s, base : base + 256]
-            X = tn(jnp.concatenate([rh, rl, rh], 0), jnp.concatenate([ch, ch, cl], 0))
-            U = X if U is None else U + X
+    U = jnp.zeros((512, 256), F32)
+    for y, yh, yl, o in ((y0, ph, pm, PS), (y1, qh, ql, 0)):
+        th, tl = split2(y[...].T)
+        U = U + nn(left3(th, tl), right3(yh[:, o : o + 256], yl[:, o : o + 256]))
     at = pl.ds(pl.multiple_of(j * 16, 16), 16)
     cols = jnp.concatenate([y0[at, :], y1[at, :], jnp.zeros((96, 512), F32)], 0).T
     rm = r % 256

time: 103 us -> 85.7 us (0.83)
  the two profiles are of different devices: /device:TPU:7 before, /device:TPU:1 now
where the time goes in v3:
time: 85.7 us; the launch traced here: 85.5 us
  Pallas kernels  83.6 us (98%)
  local copies, waits for them, and re-layouts  1.87 us (2%)
    pallas_call x1, Pallas kernels, on_device(): pl.pallas_call(kernel, out_shape=jax.ShapeDtypeStruct((512, 256), F32), i...  83.6 us
    unnamed x1, local copies, waits for them, and re-layouts  1.87 us

profile of v3, /device:TPU:1, one launch (start us, length us, event | category | flops | bytes accessed | tf_op | source)
XLA Modules:
  0.0 85.5 jit_solution(18383665459409823291)
XLA Ops:
  0.0 83.6 %refresh.1 = f32[512,256]{1,0:T(8,128)} custom-call(f32[512,256]{1,0:T(8,128)} %bitcast.3), custom_call_target="tpu_custom_call" | custom-call | tf_op jit(solution)/shard_map/refresh/pallas_call | solution.py:363
  83.6 1.9 %copy.3 = f32[1,512,256]{2,1,0:T(8,128)} copy(f32[1,512,256]{2,1,0:T(8,128)} %bitcast.2) | data formatting | bytes 1048576

commit v4 on v3

--- a/solution.py
+++ b/solution.py
@@ -9,7 +9,8 @@
 MESH = pl.DeviceIdType.MESH
 damping_share = 0.03162277660168379
 NB = 128
-MINI = 32
+MINI = 64
+AHEAD = (5, 6, 8)
 PS = 512
 RW = PS + 256 + 512
 
@@ -42,55 +43,66 @@
     return jnp.concatenate([h, h, l], axis=0)
 
 
-def block_inverse(M, b=MINI):
-    n = 128
+def block_inverse(M, b=MINI, ahead=AHEAD):
+    n = NB
     H = b // 8
     sub = lax.broadcasted_iota(jnp.int32, (8, n), 0)
     lane = lax.broadcasted_iota(jnp.int32, (8, n), 1)
-    M = [M[8 * i:8 * i + 8, :] for i in range(n // 8)]
-    for s in range(n // b):
-        r0 = s * b
+
+    def spread(x, s):
+        return jnp.broadcast_to(x[s : s + 1, :], (8, n))
+
+    M = [M[8 * q : 8 * q + 8, :] for q in range(n // 8)]
+    for r0 in range(0, n, b):
         q0 = r0 // 8
-        S = [[None] * b for _ in range(H)]
-        for k in range(b):
-            for h in range(k // 8, H):
-                S[h][k] = jnp.broadcast_to(M[q0 + h][:, r0 + k:r0 + k + 1], (8, n))
-        inblk = (lane >= r0) & (lane < r0 + b)
-        N = [jnp.where(inblk, jnp.where(lane - r0 == sub + 8 * h, 1.0, 0.0).astype(F32), M[q0 + h]) for h in range(H)]
+        N = M[q0 : q0 + H]
+
+        def column(k):
+            return [
+                jnp.broadcast_to(N[h][:, r0 + k : r0 + k + 1], (8, n)) if h >= k // 8 else None for h in range(H)]
+
+        S = {k: column(k) for k in range(ahead[0])}
+        have = ahead[0]
         scale = [None] * H
-        d = jnp.broadcast_to(S[0][0][0:1, :], (8, n))
+        d = spread(S[0][0], 0)
         for j in range(b):
             hj, sj = j // 8, j % 8
             rs = lax.rsqrt(d)
             scale[hj] = rs if sj == 0 else jnp.where(sub == sj, rs, scale[hj])
+            here = lane == r0 + j
+            N[hj] = jnp.where(here, jnp.where(sub == sj, 1.0, 0.0), N[hj])
             if j == b - 1:
                 break
-            row = [None] * b
-            for k in range(j + 1, b):
-                row[k] = jnp.broadcast_to(S[k // 8][j][k % 8 : k % 8 + 1, :], (8, n))
+            C = S.pop(j)
+            row = {k: spread(C[k // 8], k % 8) for k in S}
             rinv = rs * rs
             hn, sn = (j + 1) // 8, (j + 1) % 8
-            d = jnp.broadcast_to(S[hn][j + 1][sn : sn + 1, :], (8, n)) - (row[j + 1] * row[j + 1]) * rinv
-            u = [S[h][j] * rinv if h >= hj else None for h in range(H)]
-            for k in range(j + 1, b):
-                for h in range(k // 8, H):
-                    S[h][k] = S[h][k] - u[h] * row[k]
-            prow = jnp.broadcast_to(N[hj][sj : sj + 1, :], (8, n))
+            d = spread(S[j + 1][hn], sn) - (row[j + 1] * row[j + 1]) * rinv
+            u = [C[h] * rinv if h >= hj else None for h in range(H)]
+            for k in S:
+                S[k] = [S[k][h] - u[h] * row[k] if h >= k // 8 else None for h in range(H)]
+            prow = spread(N[hj], sj)
             for h in range(hj, H):
                 if h > hj:
-                    N[h] = N[h] - u[h] * prow
+                    N[h] = jnp.where(here, 0.0, N[h]) - u[h] * prow
                 elif sj < 7:
                     N[h] = N[h] - jnp.where(sub > sj, u[h], 0.0) * prow
-        Y = jnp.concatenate([N[h] * scale[h] for h in range(H)], axis=0)
-        lb = lax.broadcasted_iota(jnp.int32, (b, n), 1)
+            while have < min(b, j + 1 + ahead[3 * j // b]):
+                S[have] = column(have)
+                have += 1
+        N = [N[h] * scale[h] for h in range(H)]
         for h in range(H):
-            M[q0 + h] = Y[8 * h:8 * h + 8, :] if s == n // b - 1 else jnp.where(lane < r0 + b, Y[8 * h:8 * h + 8, :], 0.0)
-        if s < n // b - 1:
-            h_, m_, l_ = split3(Y)
+            M[q0 + h] = jnp.where(lane <= sub + (r0 + 8 * h), N[h], 0.0)
+        if r0 + b < n:
+            X = [
+                jnp.where((lane > sub + (r0 + 8 * h)) & (lane < r0 + b), 0.0, N[h]) for h in range(H)]
+            h_, m_, l_ = split3(jnp.concatenate(X, axis=0))
             R = tn(jnp.concatenate([h_, h_, m_, h_, l_, m_], 0), jnp.concatenate([h_, m_, h_, l_, h_, m_], 0))
+            inblk = (lane >= r0) & (lane < r0 + b)
             for q in range(q0 + H, n // 8):
-                M[q] = jnp.where(inblk, 0.0, M[q]) - R[8 * q:8 * q + 8, :]
+                M[q] = jnp.where(inblk, 0.0, M[q]) - R[8 * q : 8 * q + 8, :]
     return jnp.concatenate(M, axis=0)
+
 
 def kernel(a_ref, out_ref, akk, bc, br, zb, tz, tx, dn, wst, lh, ll, kh, kl, g0, g1, ph, pm, qh, ql, y0, y1, w_ref,
            zs, zr, zd, ts, tr, xs, xr, ks, kr, kd, hs, hr, us, ur, ds, dr):
@@ -160,17 +172,51 @@
     def h_copy(d, s):
         return copy(tx.at[s], tx.at[s], hs.at[d], hr.at[d], xpeer(d))
 
-    def strip(n, s, h):
-        return (akk.at[0, s, h, :, pl.ds(0, 512)], akk.at[0, s, h, :, pl.ds(512, 512)],
-                akk.at[1, s, h, :, pl.ds(512, 512)])[n]
-
-    def k_copy(n, d, s):
-        return copy(strip(n, s, c), strip(n, s, c), ks.at[n, d], kr.at[n, d], xpeer(d))
-
-    def k_pair(n, h):
-        v = (akk.at[0, :, h, :, pl.ds(0, 512)], akk.at[0, :, h, :, pl.ds(512, 512)],
-             akk.at[1, :, h, :, pl.ds(512, 512)])[n]
-        return copy(v, v, kd.at[n], kd.at[3 + n], partner)
+    def lanes(n, x):
+        return pl.ds(512, 512) if n == 1 else pl.ds((512 if n else 0) + NB * x, 512 - NB * x)
+
+    def k_send(n, x, d):
+        v = akk.at[n // 2, i, c, :, lanes(n, x)]
+        return copy(v, v, ks.at[n, d], kr.at[n, i], xpeer(d))
+
+    def k_sends(n, f):
+        for x in range(1 if n == 1 else 4):
+            if n == 1:
+                each(1, 16, lambda d: f(k_send(n, x, d)))
+            else:
+
+                @pl.when(i // 4 == x)
+                def _():
+                    each(1, 16, lambda d: f(k_send(n, x, d)))
+
+    def k_recv(n):
+        for x in range(4):
+
+            def one(s, carry):
+                @pl.when(s != i)
+                def _():
+                    v = akk.at[n // 2, s, c, :, lanes(n, x)]
+                    copy(v, v, ks.at[n, 0], kr.at[n, s], partner).wait_recv()
+                return carry
+
+            lax.fori_loop(4 * x, 4 * x + 4, one, 0)
+
+    def k_pair(n, x, h):
+        v = akk.at[n // 2, pl.ds(4 * x, 4), h, :, lanes(n, x)]
+        return copy(v, v, kd.at[0, n, x], kd.at[1, n, x], partner)
+
+    def k_pairs(n, h, f):
+        for x in range(4):
+            f(k_pair(n, x, h))
+
+    def begin(v):
+        v.start()
+
+    def arrived(v):
+        v.wait_recv()
+
+    def left(v):
+        v.wait_send()
 
     def z_pair(h):
         return copy(zb.at[:, h], zb.at[:, h], zd.at[0], zd.at[1], partner)
@@ -205,31 +251,30 @@
     ring(0, False).start()
     pair(z, c).start()
     each(1, 16, lambda d: x_copy(d, i).start())
-    ring_step(1)
-    ring_step(2)
     each(1, 16, lambda d: t_copy(d, behind(z, d)).wait_recv())
     t_pair(c).start()
     each(1, 16, lambda d: z_copy(d, behind(z, d)).wait_recv())
     z_pair(c).start()
-    ring_step(3)
+    ring_step(1)
     t_pair(1 - c).wait_recv()
     tx[i] = jnp.sum(tz[...].reshape(32, 1, 128), axis=0)
     each(1, 16, lambda d: h_copy(d, i).start())
     z_pair(1 - c).wait_recv()
     S = zb[...].reshape(512, 128).T
     akk[0, i, c, :, 0:512] = jnp.where(c == 0, S[0:16, :], S[32:48, :])
-    each(1, 16, lambda d: k_copy(0, d, i).start())
+    k_sends(0, begin)
     akk[0, i, c, :, 512:1024] = jnp.where(c == 0, S[64:80, :], S[96:112, :])
     akk[1, i, c, :, 512:1024] = jnp.where(c == 0, S[80:96, :], S[112:128, :])
-    ring_step(4)
+    ring_step(2)
     each(1, 16, lambda d: h_copy(d, behind(i, d)).wait_recv())
     damp = jnp.sum(tx[...], axis=0) * (damping_share / 8192.0)
-    ring_step(5)
-    each(1, 16, lambda d: k_copy(0, d, behind(i, d)).wait_recv())
-    k_pair(0, c).start()
-    each(1, 16, lambda d: k_copy(1, d, i).start())
-    each(1, 16, lambda d: k_copy(2, d, i).start())
-    k_pair(0, 1 - c).wait_recv()
+    ring_step(3)
+    k_recv(0)
+    k_pairs(0, c, begin)
+    k_sends(1, begin)
+    k_sends(2, begin)
+    ring_step(4)
+    k_pairs(0, 1 - c, arrived)
 
     damp2 = jnp.concatenate([damp, damp], axis=1)
     damp4 = jnp.concatenate([damp2, damp2], axis=1)
@@ -243,14 +288,12 @@
     dn[...] = g0[0:NB, 0:NB]
 
     def middle():
-        each(1, 16, lambda d: k_copy(1, d, behind(i, d)).wait_recv())
-        k_pair(1, c).start()
+        ring(7, True, True).wait_recv()
+        pair(lax.rem(z + 8, 16), c).start()
         each(1, 16, lambda d: x_copy(d, behind(i, d)).wait_recv())
-        each(1, 16, lambda d: k_copy(2, d, behind(i, d)).wait_recv())
-        k_pair(2, c).start()
+        k_pairs(1, 1 - c, arrived)
+        k_pairs(2, 1 - c, arrived)
         each(0, 16, lambda k: pair(k, 1 - c).wait_recv())
-        k_pair(1, 1 - c).wait_recv()
-        k_pair(2, 1 - c).wait_recv()
         for b in range(4):
             o = b * NB
             rows = slice(o, o + NB)
@@ -268,9 +311,9 @@
             th, tl = split2(Y[:, 0:PS].T)
             kh[:, o : o + NB] = th
             kl[:, o : o + NB] = tl
-        left = jnp.concatenate([kh[...], kl[...], kh[...]], axis=1)
+        lhs = jnp.concatenate([kh[...], kl[...], kh[...]], axis=1)
         for o in range(0, RW, 256):
-            R = nn(left, jnp.concatenate([ph[:, o : o + 256], ph[:, o : o + 256], pm[:, o : o + 256]], axis=0))
+            R = nn(lhs, jnp.concatenate([ph[:, o : o + 256], ph[:, o : o + 256], pm[:, o : o + 256]], axis=0))
             if o < PS:
                 src = akk[1, :, :, :, 512 + o : 768 + o].reshape(512, 256)
             elif o == PS:
@@ -294,11 +337,13 @@
                 rows = slice(kk * NB, lo)
                 if k < 4:
                     wst[k] = wl
-                    if k < 2:
-                        ring_step(6 + k)
+                    if k < 3:
+                        ring_step(5 + k)
                     if k == 2:
-                        ring(7, True, True).wait_recv()
-                        pair(lax.rem(z + 8, 16), c).start()
+                        k_recv(1)
+                        k_pairs(1, c, begin)
+                        k_recv(2)
+                        k_pairs(2, c, begin)
                     if k == 3:
                         middle()
                         return
@@ -316,11 +361,11 @@
                     if k < 4:
                         lh[lo:PS, rows] = th
                         ll[lo:PS, rows] = tl
-                    left = left3(th, tl)
+                    lhs = left3(th, tl)
                     right = right3(h, l)
                     for o in range(0, hi - lo, 256):
                         e = min(o + 256, hi - lo)
-                        g[lo:PS, lo + o : lo + e] = g[lo:PS, lo + o : lo + e] - nn(left, right[:, o:e])
+                        g[lo:PS, lo + o : lo + e] = g[lo:PS, lo + o : lo + e] - nn(lhs, right[:, o:e])
                     dn[...] = g[lo : lo + NB, lo : lo + NB]
         return carry
 
@@ -345,8 +390,8 @@
     each(1, 16, lambda d: x_copy(d, i).wait_send())
     each(1, 16, lambda d: h_copy(d, i).wait_send())
     for n in range(3):
-        each(1, 16, lambda d: k_copy(n, d, i).wait_send())
-        k_pair(n, c).wait_send()
+        k_sends(n, left)
+        k_pairs(n, c, left)
     for s in range(8):
         ring(s, True).wait_send()
         if s < 7:
@@ -372,7 +417,7 @@
             v((PS, PS), F32), v((PS, RW), F32), v((PS, RW), BF16), v((PS, RW), BF16),
             v((PS, 768), BF16), v((PS, 768), BF16), v((PS, 512), F32), v((PS, 512), F32), v((NB, NB), F32),
             dma((16,)), dma((16,)), dma((4,)), dma((16,)), dma((16,)), dma((16,)), dma((16,)),
-            dma((3, 16)), dma((3, 16)), dma((6,)), dma((16,)), dma((16,)), dma((16,)), dma((16,)),
+            dma((3, 16)), dma((3, 16)), dma((2, 3, 4)), dma((16,)), dma((16,)), dma((16,)), dma((16,)),
             dma((16,)), dma((16,)),
         ],
         compiler_params=pltpu.CompilerParams(

time: 85.7 us -> 80.8 us (0.943)
  Pallas kernels: 83.6 us -> 78.7 us
    pallas_call x1, Pallas kernels: 83.6 us -> 78.7 us  [on_device(): pl.pallas_call(kernel, out_shape=jax.ShapeDtypeStruct((512, 256), F32), i...]
where the time goes in v4:
time: 80.8 us; the launch traced here: 80.6 us
  Pallas kernels  78.7 us (97%)
  local copies, waits for them, and re-layouts  1.87 us (2%)
    pallas_call x1, Pallas kernels, on_device(): pl.pallas_call(kernel, out_shape=jax.ShapeDtypeStruct((512, 256), F32), i...  78.7 us
    unnamed x1, local copies, waits for them, and re-layouts  1.87 us

profile of v4, /device:TPU:1, one launch (start us, length us, event | category | flops | bytes accessed | tf_op | source)
XLA Modules:
  0.0 80.6 jit_solution(174888776059972499)
XLA Ops:
  0.0 78.7 %refresh.1 = f32[512,256]{1,0:T(8,128)} custom-call(f32[512,256]{1,0:T(8,128)} %bitcast.3), custom_call_target="tpu_custom_call" | custom-call | tf_op jit(solution)/shard_map/refresh/pallas_call | solution.py:408
  78.7 1.9 %copy.3 = f32[1,512,256]{2,1,0:T(8,128)} copy(f32[1,512,256]{2,1,0:T(8,128)} %bitcast.2) | data formatting | bytes 1048576

commit v5 on v4

--- a/solution.py
+++ b/solution.py
@@ -10,7 +10,7 @@
 damping_share = 0.03162277660168379
 NB = 128
 MINI = 64
-AHEAD = (5, 6, 8)
+AHEAD = (6, 6, 7)
 PS = 512
 RW = PS + 256 + 512
 
@@ -104,8 +104,8 @@
     return jnp.concatenate(M, axis=0)
 
 
-def kernel(a_ref, out_ref, akk, bc, br, zb, tz, tx, dn, wst, lh, ll, kh, kl, g0, g1, ph, pm, qh, ql, y0, y1, w_ref,
-           zs, zr, zd, ts, tr, xs, xr, ks, kr, kd, hs, hr, us, ur, ds, dr):
+def kernel(a_ref, yr, yc, damp_ref, akk, bc, br, zb, tz, tx, dn, wst, lh, ll, kh, kl, g0, g1, ph, pm,
+           w_ref, zs, zr, zd, vs, vr, ts, tr, xs, xr, ks, kr, kd, hs, hr, us, ur, ds, dr):
     i = lax.axis_index("row")
     j = lax.axis_index("col")
     z = j // 2
@@ -137,23 +137,21 @@
     each(1, 16, greet)
     pl.semaphore_signal(barrier, inc=1, device_id=partner, device_id_type=MESH)
 
-    T = a_ref[:, 0:128].T
-    br[0, z, c] = T[0:16, :]
-    br[1, z, c] = T[16:32, :]
-    lane = lax.broadcasted_iota(jnp.int32, (16, 128), 1)
-    p0, p1 = T[0:16, 0:128], T[0:16, 256:384]
-    p2, p3 = T[16:32, 0:128], T[16:32, 256:384]
-    zb[z, c] = jnp.where(
-        lane < 32, p0,
-        jnp.where(lane < 64, pltpu.roll(p1, 32, 1), jnp.where(lane < 96, pltpu.roll(p2, 64, 1), pltpu.roll(p3, 96, 1))))
-    r = lax.broadcasted_iota(jnp.int32, (512, 256), 0)
-    q = lax.broadcasted_iota(jnp.int32, (512, 256), 1)
-    on_diagonal = r + 512 * i == q + 256 * j
-    t = jnp.sum(jnp.where(on_diagonal, a_ref[...], 0.0), axis=0, keepdims=True)
+    lane = lax.broadcasted_iota(jnp.int32, (32, 128), 1)
+    V = jnp.concatenate([a_ref[0:32, 0:128], a_ref[256:288, 0:128], jnp.zeros((64, 128), F32)], 0).T[0:32, :]
+    v0 = jnp.where(lane < 16, V, pltpu.roll(V, 112, 1))
+    v1 = jnp.where(lane < 16, pltpu.roll(V, 112, 1), pltpu.roll(V, 96, 1))
+    part = lane[0:8, :]
+    zb[0, z, c] = jnp.where(
+        part < 32, v0[0:8, :],
+        jnp.where(part < 64, pltpu.roll(v0[8:16, :], 32, 1),
+                  jnp.where(part < 96, pltpu.roll(v0[16:24, :], 64, 1), pltpu.roll(v0[24:32, :], 96, 1))))
+    zb[1, z, c] = jnp.where(part < 32, v1[16:24, :], pltpu.roll(v1[24:32, :], 32, 1))
+    r = lax.broadcasted_iota(jnp.int32, (256, 256), 0)
+    q = lax.broadcasted_iota(jnp.int32, (256, 256), 1)
+    own = a_ref[pl.ds(pl.multiple_of(256 * c, 256), 256), :]
+    t = jnp.sum(jnp.where((r == q) & (z == i), own, 0.0), axis=0, keepdims=True)
     tz[z, c] = jnp.broadcast_to(jnp.sum(t, axis=1, keepdims=True), (1, 128))
-    for p in range(2):
-        for h in range(2):
-            bc[p, i, h] = a_ref[256 * h + 16 * p : 256 * h + 16 * p + 16, :]
 
     pl.semaphore_wait(barrier, 31)
 
@@ -161,7 +159,10 @@
         return lax.rem(v + 16 - d, 16)
 
     def z_copy(d, s):
-        return copy(zb.at[s, c], zb.at[s, c], zs.at[d], zr.at[d], zpeer(d))
+        return copy(zb.at[0, s, c], zb.at[0, s, c], zs.at[d], zr.at[d], zpeer(d))
+
+    def v_copy(d, s):
+        return copy(zb.at[1, s, c], zb.at[1, s, c], vs.at[d], vr.at[d], zpeer(d))
 
     def t_copy(d, s):
         return copy(tz.at[s, c], tz.at[s, c], ts.at[d], tr.at[d], zpeer(d))
@@ -219,7 +220,10 @@
         v.wait_send()
 
     def z_pair(h):
-        return copy(zb.at[:, h], zb.at[:, h], zd.at[0], zd.at[1], partner)
+        return copy(zb.at[0, :, h], zb.at[0, :, h], zd.at[0], zd.at[1], partner)
+
+    def v_pair(h):
+        return copy(zb.at[1, :, h], zb.at[1, :, h], zd.at[4], zd.at[5], partner)
 
     def t_pair(h):
         return copy(tz.at[:, h], tz.at[:, h], zd.at[2], zd.at[3], partner)
@@ -245,35 +249,52 @@
             ring(s, False).start()
         pair(lax.rem(z + s, 16), c).start()
 
+    def assembled(n):
+        p = zb[n].reshape(32, 1, 8, 128)
+        two = pltpu.roll(p.reshape(256, 128), 96, 1).reshape(32, 1, 8, 128)
+        return jnp.concatenate([p, two], axis=1).reshape(512, 128).T
+
     each(1, 16, lambda d: z_copy(d, z).start())
     each(1, 16, lambda d: t_copy(d, z).start())
+    T = a_ref[:, 0:128].T
+    br[0, z, c] = T[0:16, :]
+    br[1, z, c] = T[16:32, :]
+    for p in range(2):
+        for h in range(2):
+            bc[p, i, h] = a_ref[256 * h + 16 * p : 256 * h + 16 * p + 16, :]
     ring(0, True).start()
     ring(0, False).start()
+    each(1, 16, lambda d: v_copy(d, z).start())
     pair(z, c).start()
     each(1, 16, lambda d: x_copy(d, i).start())
+    ring_step(1)
+    each(1, 16, lambda d: z_copy(d, behind(z, d)).wait_recv())
+    z_pair(c).start()
     each(1, 16, lambda d: t_copy(d, behind(z, d)).wait_recv())
     t_pair(c).start()
-    each(1, 16, lambda d: z_copy(d, behind(z, d)).wait_recv())
-    z_pair(c).start()
-    ring_step(1)
+    ring_step(2)
+    z_pair(1 - c).wait_recv()
+    S = assembled(0)
+    akk[0, i, c, :, 0:512] = jnp.where(c == 0, S[0:16, :], S[16:32, :])
     t_pair(1 - c).wait_recv()
     tx[i] = jnp.sum(tz[...].reshape(32, 1, 128), axis=0)
     each(1, 16, lambda d: h_copy(d, i).start())
-    z_pair(1 - c).wait_recv()
-    S = zb[...].reshape(512, 128).T
-    akk[0, i, c, :, 0:512] = jnp.where(c == 0, S[0:16, :], S[32:48, :])
     k_sends(0, begin)
-    akk[0, i, c, :, 512:1024] = jnp.where(c == 0, S[64:80, :], S[96:112, :])
-    akk[1, i, c, :, 512:1024] = jnp.where(c == 0, S[80:96, :], S[112:128, :])
-    ring_step(2)
+    akk[0, i, c, :, 512:1024] = jnp.where(c == 0, S[64:80, :], S[80:96, :])
+    ring_step(3)
+    each(1, 16, lambda d: v_copy(d, behind(z, d)).wait_recv())
+    v_pair(c).start()
+    v_pair(1 - c).wait_recv()
+    S = assembled(1)
+    akk[1, i, c, :, 512:1024] = jnp.where(c == 0, S[0:16, :], S[16:32, :])
     each(1, 16, lambda d: h_copy(d, behind(i, d)).wait_recv())
     damp = jnp.sum(tx[...], axis=0) * (damping_share / 8192.0)
-    ring_step(3)
+    damp_ref[...] = jnp.broadcast_to(damp, (8, 128))
+    ring_step(4)
     k_recv(0)
     k_pairs(0, c, begin)
     k_sends(1, begin)
     k_sends(2, begin)
-    ring_step(4)
     k_pairs(0, 1 - c, arrived)
 
     damp2 = jnp.concatenate([damp, damp], axis=1)
@@ -306,7 +327,8 @@
                     jnp.concatenate([lh[rows, 0:o], ll[rows, 0:o], lh[rows, 0:o]], axis=1),
                     jnp.concatenate([ph[0:o, :], ph[0:o, :], pm[0:o, :]], axis=0))
             Y = nn(wst[b], right3(*split2(acc)))
-            y0[rows, :] = Y[:, PS + 256 :]
+            yr[rows, :] = Y[:, PS + 256 :]
+            yc[rows, :] = Y[:, PS : PS + 256]
             ph[rows, :], pm[rows, :] = split2(Y)
             th, tl = split2(Y[:, 0:PS].T)
             kh[:, o : o + NB] = th
@@ -353,9 +375,8 @@
                 Y = nn(wl, right3(*split2(g[rows, lo:hi])))
                 h, l = split2(Y)
                 if k >= 4:
-                    y1[rows, :] = Y[:, PS + 256 - lo :]
-                    qh[rows, :] = h[:, PS - lo :]
-                    ql[rows, :] = l[:, PS - lo :]
+                    yr[PS + kk * NB : PS + lo, :] = Y[:, PS + 256 - lo :]
+                    yc[PS + kk * NB : PS + lo, :] = Y[:, PS - lo : PS + 256 - lo]
                 if kk < 3:
                     th, tl = split2(Y[:, 0 : PS - lo].T)
                     if k < 4:
@@ -371,21 +392,9 @@
 
     lax.fori_loop(0, 8, body, 0)
 
-    U = jnp.zeros((512, 256), F32)
-    for y, yh, yl, o in ((y0, ph, pm, PS), (y1, qh, ql, 0)):
-        th, tl = split2(y[...].T)
-        U = U + nn(left3(th, tl), right3(yh[:, o : o + 256], yl[:, o : o + 256]))
-    at = pl.ds(pl.multiple_of(j * 16, 16), 16)
-    cols = jnp.concatenate([y0[at, :], y1[at, :], jnp.zeros((96, 512), F32)], 0).T
-    rm = r % 256
-    posrow = jnp.where(rm < 32, (rm // 16) * 512 + (2 * i + r // 256) * 16 + rm % 16, 1024)
-    poscol = (q // 16) * 512 + j * 16 + q % 16
-    A = a_ref[...] + jnp.where(on_diagonal, damp2, 0.0)
-    cols = jnp.concatenate([cols, jnp.zeros((512, 128), F32)], 1)
-    out_ref[...] = jnp.where(
-        q >= 32, jnp.where(rm >= 32, A - U, 0.0), jnp.where(posrow >= poscol, cols, 0.0))
-
     each(1, 16, lambda d: z_copy(d, z).wait_send())
+    each(1, 16, lambda d: v_copy(d, z).wait_send())
+    v_pair(c).wait_send()
     each(1, 16, lambda d: t_copy(d, z).wait_send())
     each(1, 16, lambda d: x_copy(d, i).wait_send())
     each(1, 16, lambda d: h_copy(d, i).wait_send())
@@ -401,29 +410,60 @@
     t_pair(c).wait_send()
 
 
+def finish(a_ref, yr, yc, damp_ref, out_ref):
+    i = lax.axis_index("row")
+    j = lax.axis_index("col")
+    r = lax.broadcasted_iota(jnp.int32, (512, 256), 0)
+    q = lax.broadcasted_iota(jnp.int32, (512, 256), 1)
+    U = jnp.zeros((512, 256), F32)
+    for o in (0, PS):
+        th, tl = split2(yr[o : o + PS, :].T)
+        U = U + nn(left3(th, tl), right3(*split2(yc[o : o + PS, :])))
+    at = [pl.ds(pl.multiple_of(j * 16 + o, 16), 16) for o in (0, PS)]
+    cols = jnp.concatenate([yr[at[0], :], yr[at[1], :], jnp.zeros((96, 512), F32)], 0).T
+    rm = r % 256
+    posrow = jnp.where(rm < 32, (rm // 16) * 512 + (2 * i + r // 256) * 16 + rm % 16, 1024)
+    poscol = (q // 16) * 512 + j * 16 + q % 16
+    damp = damp_ref[0:1, :]
+    damp2 = jnp.concatenate([damp, damp], axis=1)
+    A = a_ref[...] + jnp.where(r + 512 * i == q + 256 * j, damp2, 0.0)
+    cols = jnp.concatenate([cols, jnp.zeros((512, 128), F32)], 1)
+    out_ref[...] = jnp.where(
+        q >= 32, jnp.where(rm >= 32, A - U, 0.0), jnp.where(posrow >= poscol, cols, 0.0))
+
+
 def on_device(factors):
     vm = pl.BlockSpec(memory_space=pltpu.VMEM)
     dma = pltpu.SemaphoreType.DMA
     v = pltpu.VMEM
-    out = pl.pallas_call(
+    f = jax.ShapeDtypeStruct
+    parts = pl.pallas_call(
         kernel,
-        out_shape=jax.ShapeDtypeStruct((512, 256), F32),
+        out_shape=[f((1024, 512), F32), f((1024, 256), F32), f((8, 128), F32)],
         in_specs=[vm],
-        out_specs=vm,
+        out_specs=[vm] * 3,
         scratch_shapes=[
-            v((2, 16, 2, 16, 1024), F32), v((2, 16, 2, 16, 256), F32), v((2, 16, 2, 16, 512), F32),
-            v((16, 2, 16, 128), F32), v((16, 2, 1, 128), F32), v((16, 1, 128), F32),
-            v((NB, NB), F32), v((4, NB, 3 * NB), BF16), v((PS, PS), BF16), v((PS, PS), BF16), v((PS, PS), BF16), v((PS, PS), BF16),
-            v((PS, PS), F32), v((PS, RW), F32), v((PS, RW), BF16), v((PS, RW), BF16),
-            v((PS, 768), BF16), v((PS, 768), BF16), v((PS, 512), F32), v((PS, 512), F32), v((NB, NB), F32),
-            dma((16,)), dma((16,)), dma((4,)), dma((16,)), dma((16,)), dma((16,)), dma((16,)),
+            v((2, 16, 2, 16, 1024), F32), v((2, 16, 2, 16, 256), F32),
+            v((2, 16, 2, 16, 512), F32), v((2, 16, 2, 8, 128), F32), v((16, 2, 1, 128), F32), v((16, 1, 128), F32),
+            v((NB, NB), F32), v((4, NB, 3 * NB), BF16), v((PS, PS), BF16), v((PS, PS), BF16), v((PS, PS), BF16),
+            v((PS, PS), BF16), v((PS, PS), F32), v((PS, RW), F32), v((PS, RW), BF16), v((PS, RW), BF16),
+            v((NB, NB), F32),
+            dma((16,)), dma((16,)), dma((6,)), dma((16,)), dma((16,)), dma((16,)), dma((16,)), dma((16,)), dma((16,)),
             dma((3, 16)), dma((3, 16)), dma((2, 3, 4)), dma((16,)), dma((16,)), dma((16,)), dma((16,)),
             dma((16,)), dma((16,)),
         ],
         compiler_params=pltpu.CompilerParams(
-            collective_id=0, has_side_effects=True, vmem_limit_bytes=56 * 1024 * 1024),
-        name="refresh",
+            collective_id=0, has_side_effects=True, vmem_limit_bytes=42 * 1024 * 1024),
+        name="gather_eliminate",
     )(factors[0])
+    out = pl.pallas_call(
+        finish,
+        out_shape=f((512, 256), F32),
+        in_specs=[vm] * 4,
+        out_specs=vm,
+        compiler_params=pltpu.CompilerParams(vmem_limit_bytes=16 * 1024 * 1024),
+        name="finish",
+    )(factors[0], *parts)
     return out[None]
 
 

time: 80.8 us -> 76.9 us (0.952)
  Pallas kernels: 78.7 us -> 75.7 us
  local copies, waits for them, and re-layouts: 1.87 us -> 1.04 us
    pallas_call x1 -> x2, Pallas kernels: 78.7 us -> 75.7 us  [the longest x1 73.5 us: on_device(): pl.pallas_call(kernel, out_shape=[f((1024, 512), F32), f((1024, 256), F32...]
    unnamed x1 -> x2, local copies, waits for them, and re-layouts: 1.87 us -> 1.04 us
where the time goes in v5:
time: 76.9 us; the launch traced here: 76.8 us
  Pallas kernels  75.7 us (98%)
  local copies, waits for them, and re-layouts  1.04 us (1%)
    pallas_call x1, Pallas kernels, on_device(): pl.pallas_call(kernel, out_shape=[f((1024, 512), F32), f((1024, 256), F32...  73.5 us
    pallas_call x1, Pallas kernels, on_device(): pl.pallas_call(finish, out_shape=f((512, 256), F32), in_specs=[vm] * 4, o...  2.23 us

profile of v5, /device:TPU:1, one launch (start us, length us, event | category | flops | bytes accessed | tf_op | source)
XLA Modules:
  0.0 76.8 jit_solution(17985096243585248180)
XLA Ops:
  0.0 0.0 copy-start
  0.0 1.0 %copy-done = f32[1,512,256]{2,1,0:T(8,128)S(1)} copy-done((f32[1,512,256]{2,1,0:T(8,128)S(1)}, f32[1,512,256]{2,1,0:T(8,128)}, u32[]{:S(2)}) %copy-start) | copy-done | bytes 524312
  1.0 73.5 %gather_eliminate.1 = (f32[1024,512]{1,0:T(8,128)S(1)}, f32[1024,256]{1,0:T(8,128)S(1)}, f32[8,128]{1,0:T(8,128)S(1)}) custom-call(f32[512,256]{1,0:T(8,128)S(1)} %bitcast.2), custom_call_target="tpu_custom_call" | custom-call | tf_op jit(solution)/shard_map/gather_eliminate/pallas_call | solution.py:440
  74.5 2.2 %finish.1 = f32[512,256]{1,0:T(8,128)} custom-call(f32[512,256]{1,0:T(8,128)S(1)} %bitcast.3, f32[1024,512]{1,0:T(8,128)S(1)} %get-tuple-element.8.yr, f32[1024,256]{1,0:T(8,128)S(1)} %get-tuple-element.9.yc, f32[8,128]{1,0:T(8,128)S(1)} %get-tuple-element.10.damp_ref), custom_call_target="tpu_custom_call" | custom-call | tf_op jit(solution)/shard_map/finish/pallas_call | solution.py:459
Async XLA Ops:
  0.0 1.0 %copy-start = (f32[1,512,256]{2,1,0:T(8,128)S(1)}, f32[1,512,256]{2,1,0:T(8,128)}, u32[]{:S(2)}) copy-start(f32[1,512,256]{2,1,0:T(8,128)} %param.1) | copy-start | bytes 1572868

commit v6 on v5

--- a/solution.py
+++ b/solution.py
@@ -190,8 +190,8 @@
                 def _():
                     each(1, 16, lambda d: f(k_send(n, x, d)))
 
-    def k_recv(n):
-        for x in range(4):
+    def k_recv(n, xs=(0, 1, 2, 3)):
+        for x in xs:
 
             def one(s, carry):
                 @pl.when(s != i)
@@ -235,19 +235,27 @@
         e = s + 1 if arriving else s
         k = behind(z, e) if up else lax.rem(z + e, 16)
         o = 0 if up else 8
-        return copy(br.at[:, k, c], br.at[:, k, c], us.at[s + o], ur.at[s + o], up_to if up else down_to)
+        return [
+            copy(br.at[p, k, c], br.at[p, k, c], us.at[p, s + o], ur.at[p, s + o], up_to if up else down_to)
+            for p in range(2)]
 
     def pair(k, h):
         return copy(br.at[:, k, h], br.at[:, k, h], ds.at[k], dr.at[k], partner)
 
     def ring_step(s):
-        ring(s - 1, True, True).wait_recv()
-        ring(s, True).start()
+        for p in range(2):
+            ring(s - 1, True, True)[p].wait_recv()
+            ring(s, True)[p].start()
+            ring(s - 1, False, True)[p].wait_recv()
+            if s < 7:
+                ring(s, False)[p].start()
         pair(behind(z, s), c).start()
-        ring(s - 1, False, True).wait_recv()
-        if s < 7:
-            ring(s, False).start()
         pair(lax.rem(z + s, 16), c).start()
+
+    def ring_end():
+        for p in range(2):
+            ring(7, True, True)[p].wait_recv()
+        pair(lax.rem(z + 8, 16), c).start()
 
     def assembled(n):
         p = zb[n].reshape(32, 1, 8, 128)
@@ -262,17 +270,17 @@
     for p in range(2):
         for h in range(2):
             bc[p, i, h] = a_ref[256 * h + 16 * p : 256 * h + 16 * p + 16, :]
-    ring(0, True).start()
-    ring(0, False).start()
+    for p in range(2):
+        ring(0, True)[p].start()
+        ring(0, False)[p].start()
     each(1, 16, lambda d: v_copy(d, z).start())
     pair(z, c).start()
     each(1, 16, lambda d: x_copy(d, i).start())
-    ring_step(1)
     each(1, 16, lambda d: z_copy(d, behind(z, d)).wait_recv())
     z_pair(c).start()
     each(1, 16, lambda d: t_copy(d, behind(z, d)).wait_recv())
     t_pair(c).start()
-    ring_step(2)
+    ring_step(1)
     z_pair(1 - c).wait_recv()
     S = assembled(0)
     akk[0, i, c, :, 0:512] = jnp.where(c == 0, S[0:16, :], S[16:32, :])
@@ -280,22 +288,26 @@
     tx[i] = jnp.sum(tz[...].reshape(32, 1, 128), axis=0)
     each(1, 16, lambda d: h_copy(d, i).start())
     k_sends(0, begin)
+    ring_step(2)
     akk[0, i, c, :, 512:1024] = jnp.where(c == 0, S[64:80, :], S[80:96, :])
-    ring_step(3)
     each(1, 16, lambda d: v_copy(d, behind(z, d)).wait_recv())
     v_pair(c).start()
     v_pair(1 - c).wait_recv()
+    ring_step(3)
     S = assembled(1)
     akk[1, i, c, :, 512:1024] = jnp.where(c == 0, S[0:16, :], S[16:32, :])
     each(1, 16, lambda d: h_copy(d, behind(i, d)).wait_recv())
     damp = jnp.sum(tx[...], axis=0) * (damping_share / 8192.0)
     damp_ref[...] = jnp.broadcast_to(damp, (8, 128))
-    ring_step(4)
-    k_recv(0)
-    k_pairs(0, c, begin)
+    k_recv(0, (0,))
+    k_pair(0, 0, c).start()
+    k_recv(0, (1, 2, 3))
+    for x in (1, 2, 3):
+        k_pair(0, x, c).start()
     k_sends(1, begin)
     k_sends(2, begin)
-    k_pairs(0, 1 - c, arrived)
+    ring_step(4)
+    k_pair(0, 0, 1 - c).wait_recv()
 
     damp2 = jnp.concatenate([damp, damp], axis=1)
     damp4 = jnp.concatenate([damp2, damp2], axis=1)
@@ -305,12 +317,10 @@
     posl = jnp.where(ln % 256 < 32, (ln % 256 // 16) * 512 + (2 * i + ln // 256) * 16 + ln % 16, -1)
     posr = lax.broadcasted_iota(jnp.int32, (PS, 512), 0)
 
-    g0[...] = akk[0, :, :, :, 0:512].reshape(512, 512)
-    dn[...] = g0[0:NB, 0:NB]
+    dn[...] = akk[0, 0:4, :, :, 0:NB].reshape(NB, NB)
 
     def middle():
-        ring(7, True, True).wait_recv()
-        pair(lax.rem(z + 8, 16), c).start()
+        ring_end()
         each(1, 16, lambda d: x_copy(d, behind(i, d)).wait_recv())
         k_pairs(1, 1 - c, arrived)
         k_pairs(2, 1 - c, arrived)
@@ -361,6 +371,10 @@
                     wst[k] = wl
                     if k < 3:
                         ring_step(5 + k)
+                    if k == 0:
+                        for x in (1, 2, 3):
+                            k_pair(0, x, 1 - c).wait_recv()
+                        g0[...] = akk[0, :, :, :, 0:512].reshape(512, 512)
                     if k == 2:
                         k_recv(1)
                         k_pairs(1, c, begin)
@@ -402,9 +416,10 @@
         k_sends(n, left)
         k_pairs(n, c, left)
     for s in range(8):
-        ring(s, True).wait_send()
-        if s < 7:
-            ring(s, False).wait_send()
+        for p in range(2):
+            ring(s, True)[p].wait_send()
+            if s < 7:
+                ring(s, False)[p].wait_send()
     each(0, 16, lambda k: pair(k, c).wait_send())
     z_pair(c).wait_send()
     t_pair(c).wait_send()
@@ -449,7 +464,7 @@
             v((PS, PS), BF16), v((PS, PS), F32), v((PS, RW), F32), v((PS, RW), BF16), v((PS, RW), BF16),
             v((NB, NB), F32),
             dma((16,)), dma((16,)), dma((6,)), dma((16,)), dma((16,)), dma((16,)), dma((16,)), dma((16,)), dma((16,)),
-            dma((3, 16)), dma((3, 16)), dma((2, 3, 4)), dma((16,)), dma((16,)), dma((16,)), dma((16,)),
+            dma((3, 16)), dma((3, 16)), dma((2, 3, 4)), dma((16,)), dma((16,)), dma((2, 16)), dma((2, 16)),
             dma((16,)), dma((16,)),
         ],
         compiler_params=pltpu.CompilerParams(

time: 76.9 us -> 76.6 us (level)
  no operation moved by 1% of the time
where the time goes in v6:
time: 76.6 us; the launch traced here: 76.5 us
  Pallas kernels  75.4 us (98%)
  local copies, waits for them, and re-layouts  1.04 us (1%)
    pallas_call x1, Pallas kernels, on_device(): pl.pallas_call(kernel, out_shape=[f((1024, 512), F32), f((1024, 256), F32...  73.2 us
    pallas_call x1, Pallas kernels, on_device(): pl.pallas_call(finish, out_shape=f((512, 256), F32), in_specs=[vm] * 4, o...  2.23 us

profile of v6, /device:TPU:1, one launch (start us, length us, event | category | flops | bytes accessed | tf_op | source)
XLA Modules:
  0.0 76.5 jit_solution(13201523908914902022)
XLA Ops:
  0.0 0.0 copy-start
  0.0 1.0 %copy-done = f32[1,512,256]{2,1,0:T(8,128)S(1)} copy-done((f32[1,512,256]{2,1,0:T(8,128)S(1)}, f32[1,512,256]{2,1,0:T(8,128)}, u32[]{:S(2)}) %copy-start) | copy-done | bytes 524312
  1.0 73.2 %gather_eliminate.1 = (f32[1024,512]{1,0:T(8,128)S(1)}, f32[1024,256]{1,0:T(8,128)S(1)}, f32[8,128]{1,0:T(8,128)S(1)}) custom-call(f32[512,256]{1,0:T(8,128)S(1)} %bitcast.2), custom_call_target="tpu_custom_call" | custom-call | tf_op jit(solution)/shard_map/gather_eliminate/pallas_call | solution.py:455
  74.2 2.2 %finish.1 = f32[512,256]{1,0:T(8,128)} custom-call(f32[512,256]{1,0:T(8,128)S(1)} %bitcast.3, f32[1024,512]{1,0:T(8,128)S(1)} %get-tuple-element.8.yr, f32[1024,256]{1,0:T(8,128)S(1)} %get-tuple-element.9.yc, f32[8,128]{1,0:T(8,128)S(1)} %get-tuple-element.10.damp_ref), custom_call_target="tpu_custom_call" | custom-call | tf_op jit(solution)/shard_map/finish/pallas_call | solution.py:474
Async XLA Ops:
  0.0 1.0 %copy-start = (f32[1,512,256]{2,1,0:T(8,128)S(1)}, f32[1,512,256]{2,1,0:T(8,128)}, u32[]{:S(2)}) copy-start(f32[1,512,256]{2,1,0:T(8,128)} %param.1) | copy-start | bytes 1572868

commit v7 on v6

--- a/solution.py
+++ b/solution.py
@@ -116,7 +116,10 @@
         return (i, 2 * lax.rem(z + d, 16) + c)
 
     def xpeer(d):
-        return (lax.rem(i + d, 16), j)
+        return (4 * lax.rem(i // 4 + d // 4, 4) + lax.rem(i + d, 4), j)
+
+    def xfrom(d):
+        return 4 * lax.rem(i // 4 + 4 - d // 4, 4) + lax.rem(i + 4 - lax.rem(d, 4), 4)
 
     def copy(src, dst, ssem, rsem, dev):
         return pltpu.make_async_remote_copy(
@@ -296,16 +299,16 @@
     ring_step(3)
     S = assembled(1)
     akk[1, i, c, :, 512:1024] = jnp.where(c == 0, S[0:16, :], S[16:32, :])
-    each(1, 16, lambda d: h_copy(d, behind(i, d)).wait_recv())
+    each(1, 16, lambda d: h_copy(d, xfrom(d)).wait_recv())
     damp = jnp.sum(tx[...], axis=0) * (damping_share / 8192.0)
     damp_ref[...] = jnp.broadcast_to(damp, (8, 128))
     k_recv(0, (0,))
     k_pair(0, 0, c).start()
+    k_sends(1, begin)
+    k_sends(2, begin)
     k_recv(0, (1, 2, 3))
     for x in (1, 2, 3):
         k_pair(0, x, c).start()
-    k_sends(1, begin)
-    k_sends(2, begin)
     ring_step(4)
     k_pair(0, 0, 1 - c).wait_recv()
 
@@ -320,8 +323,7 @@
     dn[...] = akk[0, 0:4, :, :, 0:NB].reshape(NB, NB)
 
     def middle():
-        ring_end()
-        each(1, 16, lambda d: x_copy(d, behind(i, d)).wait_recv())
+        each(1, 16, lambda d: x_copy(d, xfrom(d)).wait_recv())
         k_pairs(1, 1 - c, arrived)
         k_pairs(2, 1 - c, arrived)
         each(0, 16, lambda k: pair(k, 1 - c).wait_recv())
@@ -380,6 +382,7 @@
                         k_pairs(1, c, begin)
                         k_recv(2)
                         k_pairs(2, c, begin)
+                        ring_end()
                     if k == 3:
                         middle()
                         return

time: 76.6 us -> 76.6 us (level)
  no operation moved by 1% of the time
where the time goes in v7:
time: 76.6 us; the launch traced here: 76.4 us
  Pallas kernels  75.4 us (98%)
  local copies, waits for them, and re-layouts  1.04 us (1%)
    pallas_call x1, Pallas kernels, on_device(): pl.pallas_call(kernel, out_shape=[f((1024, 512), F32), f((1024, 256), F32...  73.2 us
    pallas_call x1, Pallas kernels, on_device(): pl.pallas_call(finish, out_shape=f((512, 256), F32), in_specs=[vm] * 4, o...  2.23 us

profile of v7, /device:TPU:1, one launch (start us, length us, event | category | flops | bytes accessed | tf_op | source)
XLA Modules:
  0.0 76.4 jit_solution(5632729479563790358)
XLA Ops:
  0.0 0.0 copy-start
  0.0 1.0 %copy-done = f32[1,512,256]{2,1,0:T(8,128)S(1)} copy-done((f32[1,512,256]{2,1,0:T(8,128)S(1)}, f32[1,512,256]{2,1,0:T(8,128)}, u32[]{:S(2)}) %copy-start) | copy-done | bytes 524312
  1.0 73.2 %gather_eliminate.1 = (f32[1024,512]{1,0:T(8,128)S(1)}, f32[1024,256]{1,0:T(8,128)S(1)}, f32[8,128]{1,0:T(8,128)S(1)}) custom-call(f32[512,256]{1,0:T(8,128)S(1)} %bitcast.2), custom_call_target="tpu_custom_call" | custom-call | tf_op jit(solution)/shard_map/gather_eliminate/pallas_call | solution.py:458
  74.2 2.2 %finish.1 = f32[512,256]{1,0:T(8,128)} custom-call(f32[512,256]{1,0:T(8,128)S(1)} %bitcast.3, f32[1024,512]{1,0:T(8,128)S(1)} %get-tuple-element.8.yr, f32[1024,256]{1,0:T(8,128)S(1)} %get-tuple-element.9.yc, f32[8,128]{1,0:T(8,128)S(1)} %get-tuple-element.10.damp_ref), custom_call_target="tpu_custom_call" | custom-call | tf_op jit(solution)/shard_map/finish/pallas_call | solution.py:477
Async XLA Ops:
  0.0 1.0 %copy-start = (f32[1,512,256]{2,1,0:T(8,128)S(1)}, f32[1,512,256]{2,1,0:T(8,128)}, u32[]{:S(2)}) copy-start(f32[1,512,256]{2,1,0:T(8,128)} %param.1) | copy-start | bytes 1572868

commit v8 on v6

--- a/solution.py
+++ b/solution.py
@@ -320,7 +320,6 @@
     dn[...] = akk[0, 0:4, :, :, 0:NB].reshape(NB, NB)
 
     def middle():
-        ring_end()
         each(1, 16, lambda d: x_copy(d, behind(i, d)).wait_recv())
         k_pairs(1, 1 - c, arrived)
         k_pairs(2, 1 - c, arrived)
@@ -379,6 +378,7 @@
                         k_recv(1)
                         k_pairs(1, c, begin)
                         k_recv(2)
+                        ring_end()
                         k_pairs(2, c, begin)
                     if k == 3:
                         middle()

time: 76.6 us -> 77.1 us (level)
  no operation moved by 1% of the time
where the time goes in v8:
time: 77.1 us; the launch traced here: 76.9 us
  Pallas kernels  75.9 us (98%)
  local copies, waits for them, and re-layouts  1.04 us (1%)
    pallas_call x1, Pallas kernels, on_device(): pl.pallas_call(kernel, out_shape=[f((1024, 512), F32), f((1024, 256), F32...  73.6 us
    pallas_call x1, Pallas kernels, on_device(): pl.pallas_call(finish, out_shape=f((512, 256), F32), in_specs=[vm] * 4, o...  2.23 us

profile of v8, /device:TPU:1, one launch (start us, length us, event | category | flops | bytes accessed | tf_op | source)
XLA Modules:
  0.0 76.9 jit_solution(15626807271356692172)
XLA Ops:
  0.0 0.0 copy-start
  0.0 1.0 %copy-done = f32[1,512,256]{2,1,0:T(8,128)S(1)} copy-done((f32[1,512,256]{2,1,0:T(8,128)S(1)}, f32[1,512,256]{2,1,0:T(8,128)}, u32[]{:S(2)}) %copy-start) | copy-done | bytes 524312
  1.0 73.6 %gather_eliminate.1 = (f32[1024,512]{1,0:T(8,128)S(1)}, f32[1024,256]{1,0:T(8,128)S(1)}, f32[8,128]{1,0:T(8,128)S(1)}) custom-call(f32[512,256]{1,0:T(8,128)S(1)} %bitcast.2), custom_call_target="tpu_custom_call" | custom-call | tf_op jit(solution)/shard_map/gather_eliminate/pallas_call | solution.py:455
  74.7 2.2 %finish.1 = f32[512,256]{1,0:T(8,128)} custom-call(f32[512,256]{1,0:T(8,128)S(1)} %bitcast.3, f32[1024,512]{1,0:T(8,128)S(1)} %get-tuple-element.8.yr, f32[1024,256]{1,0:T(8,128)S(1)} %get-tuple-element.9.yc, f32[8,128]{1,0:T(8,128)S(1)} %get-tuple-element.10.damp_ref), custom_call_target="tpu_custom_call" | custom-call | tf_op jit(solution)/shard_map/finish/pallas_call | solution.py:474
Async XLA Ops:
  0.0 1.0 %copy-start = (f32[1,512,256]{2,1,0:T(8,128)S(1)}, f32[1,512,256]{2,1,0:T(8,128)}, u32[]{:S(2)}) copy-start(f32[1,512,256]{2,1,0:T(8,128)} %param.1) | copy-start | bytes 1572868
